TPU v7x, 32 devices: a whole 2x2x4 slice. The times are simulated.
32 devices in a mesh: dp: 2 (over x), tp: 4 (over z), cp: 4 (over y, core).
Axes of the slice: x: 2, y: 2, z: 4, core: 2. Of those that a mesh axis runs over, the one named last changes fastest.
Arguments:
- hidden: bfloat16 [6, 1536, 5120], P('dp', 'cp'), parts along dimension 0
- positions: int32 [6, 1536], P('dp', 'cp'), parts along dimension 0
- w_dq: bfloat16 [5120, 1536], replicated
- g_q: float32 [1536], replicated
- w_uq: bfloat16 [1536, 24576], P(None, 'tp')
- w_dkv: bfloat16 [5120, 576], replicated
- g_kv: float32 [512], replicated
- w_uk: bfloat16 [512, 16384], P(None, 'tp')
- w_uv: bfloat16 [512, 16384], P(None, 'tp')
- w_o: bfloat16 [16384, 5120], P('tp')
Outputs:
- output 1: bfloat16 [6, 1536, 5120], P('dp', 'cp'), parts along dimension 0
- output 2: bfloat16 [6, 1536, 512], P('dp', 'cp'), parts along dimension 0
- output 3: bfloat16 [6, 1536, 64], P('dp', 'cp'), parts along dimension 0
There are 2 independent parts. A program takes and returns all parts, laid end to end along the dimension named above; an argument that names none is the same for every part.
All inputs are finite; a program needn't handle non-finite values.
Results may differ from a plain program's by a relative error of at most 0.0075555.
Values are sent between devices in bfloat16 or wider.
A program may use at most 1 GiB of HBM per device.

v0:
```python
import jax
import jax.numpy as jnp
from jax import lax
from jax.sharding import PartitionSpec as P

ROPE_BASE = 10000.0
NORM_EPS = 1e-6


def rms_norm(tensor, norm_gain):
    tensor_f32 = tensor.astype(jnp.float32)
    inv_rms = lax.rsqrt(jnp.mean(tensor_f32 * tensor_f32, axis=-1, keepdims=True) + NORM_EPS)
    return (tensor_f32 * inv_rms * norm_gain).astype(jnp.bfloat16)


def rope_tables(positions, rope_dim):
    inv_freq = ROPE_BASE ** (-2.0 * jnp.arange(rope_dim // 2, dtype=jnp.float32) / rope_dim)
    angles = positions.astype(jnp.float32)[..., None] * inv_freq
    return jnp.cos(angles), jnp.sin(angles)


def rotate(tensor, cos_t, sin_t):
    tensor_f32 = tensor.astype(jnp.float32)
    half_dim = tensor_f32.shape[-1] // 2
    lower_half = tensor_f32[..., :half_dim]
    upper_half = tensor_f32[..., half_dim:]
    return jnp.concatenate([lower_half * cos_t - upper_half * sin_t,
                            lower_half * sin_t + upper_half * cos_t], axis=-1).astype(jnp.bfloat16)


def attend(q_nope, q_rope, pos_q, k_nope, k_rope, values, pos_k, soft_scale):
    scores = (jnp.einsum('nshd,nthd->nhst', q_nope, k_nope, preferred_element_type=jnp.float32)
              + jnp.einsum('nshd,ntd->nhst', q_rope, k_rope, preferred_element_type=jnp.float32)) * soft_scale
    allowed = pos_k[:, None, None, :] <= pos_q[:, None, :, None]
    scores = jnp.where(allowed, scores, -jnp.inf)
    probs_bf = jax.nn.softmax(scores, axis=-1).astype(jnp.bfloat16)
    attn_heads = jnp.einsum('nhst,nthd->nshd', probs_bf, values,
                            preferred_element_type=jnp.float32).astype(jnp.bfloat16)
    return attn_heads.reshape(attn_heads.shape[0], attn_heads.shape[1], -1)


def solution(mesh):
    def local_step(x_blk, pos_blk, w_dq, g_q, w_uq, w_dkv, g_kv, w_uk, w_uv, w_o):
        num_seq = x_blk.shape[0]
        seq_dev = x_blk.shape[1]
        kv_rank = g_kv.shape[0]
        rope_dim = w_dkv.shape[1] - kv_rank
        heads_dev = (w_uq.shape[1] - w_uk.shape[1]) // rope_dim
        nope_dim = w_uk.shape[1] // heads_dev
        v_dim = w_uv.shape[1] // heads_dev
        soft_scale = (nope_dim + rope_dim) ** -0.5
        cos_t, sin_t = rope_tables(pos_blk, rope_dim)
        q_latent = jnp.einsum('nsd,dr->nsr', x_blk, w_dq, preferred_element_type=jnp.float32).astype(jnp.bfloat16)
        q_full = jnp.einsum('nsr,rk->nsk', rms_norm(q_latent, g_q), w_uq,
                            preferred_element_type=jnp.float32).astype(jnp.bfloat16)
        q_full = q_full.reshape(num_seq, seq_dev, heads_dev, nope_dim + rope_dim)
        q_nope = q_full[..., :nope_dim]
        q_rope = rotate(q_full[..., nope_dim:], cos_t[:, :, None, :], sin_t[:, :, None, :])
        kv_joint = jnp.einsum('nsd,dc->nsc', x_blk, w_dkv, preferred_element_type=jnp.float32).astype(jnp.bfloat16)
        latent = rms_norm(kv_joint[..., :kv_rank], g_kv)
        k_rope = rotate(kv_joint[..., kv_rank:], cos_t, sin_t)
        k_nope = jnp.einsum('nsc,ck->nsk', latent, w_uk, preferred_element_type=jnp.float32).astype(jnp.bfloat16)
        k_nope = k_nope.reshape(num_seq, seq_dev, heads_dev, nope_dim)
        values = jnp.einsum('nsc,ck->nsk', latent, w_uv, preferred_element_type=jnp.float32).astype(jnp.bfloat16)
        values = values.reshape(num_seq, seq_dev, heads_dev, v_dim)
        k_nope_all = lax.all_gather(k_nope, 'cp', axis=1, tiled=True)
        values_all = lax.all_gather(values, 'cp', axis=1, tiled=True)
        k_rope_all = lax.all_gather(k_rope, 'cp', axis=1, tiled=True)
        pos_all = lax.all_gather(pos_blk, 'cp', axis=1, tiled=True)
        attn_out = attend(q_nope, q_rope, pos_blk, k_nope_all, k_rope_all, values_all, pos_all, soft_scale)
        part_out = jnp.einsum('nsk,kd->nsd', attn_out, w_o, preferred_element_type=jnp.float32)
        head_sum = lax.psum(part_out, 'tp')
        out_hidden = (x_blk.astype(jnp.float32) + head_sum).astype(jnp.bfloat16)
        return out_hidden, latent, k_rope

    seq_spec = P('dp', 'cp', None)
    in_specs = (seq_spec, P('dp', 'cp'), P(None, None), P(None), P(None, 'tp'), P(None, None), P(None),
                P(None, 'tp'), P(None, 'tp'), P('tp', None))
    return jax.shard_map(local_step, mesh=mesh, in_specs=in_specs,
                         out_specs=(seq_spec, seq_spec, seq_spec), check_vma=False)
```

profile of v0, /device:TPU:0, one launch (start us, length us, event | category | flops | bytes accessed | tf_op | source)
XLA Modules:
  0.0 1442.6 jit_solution(4812572460946690729)
XLA Ops:
  7.2 0.0 all-gather.5.cloned.1.call-start
  7.2 11.9 fusion.35
  19.1 0.2 fusion.32
  19.4 0.3 fusion.34
  19.7 7.6 convert_bitcast_fusion
  27.3 9.9 copy.40
  37.3 0.0 all-gather.5.cloned.1.call-update
  37.3 0.0 all-gather.3.cloned.1.call-start
  37.3 9.4 convolution_convert_fusion
  46.7 12.7 copy.36
  59.4 0.0 all-gather.3.cloned.1.call-update
  59.4 0.2 all-reduce.2.cloned.1.call-start
  59.6 0.4 copy-done.3
  60.1 25.1 %fusion.14 = (f32[3,384]{1,0:T(4,128)S(1)}, bf16[3,384,1536]{2,1,0:T(8,128)(2,1)S(1)}) fusion(bf16[3,384,5120]{2,1,0:T(8,128)(2,1)} %param.10, bf16[5120,1536]{1,0:T(8,128)(2,1)} %param.12), kind=kOutput, calls=%fused_computation.21 | convolution fusion | flops 18126469120 | bytes 31068672 | tf_op jit(solution)/shard_map/nsd,dr->nsr/dot_general | solution.py:53
  85.2 27.7 %fusion.10 = bf16[3,384,6144]{2,1,0:T(8,128)(2,1)} fusion(bf16[1536,6144]{1,0:T(8,128)(2,1)} %param.14, bf16[3,384,1536]{2,1,0:T(8,128)(2,1)S(1)} %get-tuple-element.16, f32[1536]{0:T(1024)S(1)} %copy-done.6, f32[3,384]{1,0:T(4,128)S(1)} %add_rsqrt_fusion), kind=kOutput, calls=%fused_computation.14 | convolution fusion | flops 21757427712 | bytes 36579840 | tf_op jit(solution)/shard_map/nsr,rk->nsk/dot_general | solution.py:54
  112.9 18.6 %copy.24 = bf16[3,384,6144]{1,2,0:T(8,128)(2,1)} copy(bf16[3,384,6144]{2,1,0:T(8,128)(2,1)} %fusion.10) | data formatting | bytes 28311552 | tf_op jit(solution)/shard_map/convert_element_type | solution.py:55
  131.6 6.4 all_gather.13
  138.0 0.6 subtract_convert_fusion.1
  138.7 11.7 all_gather.15
  150.4 3.7 slice_convert_fusion
  154.1 3.0 subtract_convert_fusion
  157.2 1.1 broadcast_compare_fusion
  158.2 74.9 %fusion.20 = f32[3,1536,384,32]{1,2,3,0:T(8,128)} fusion(bf16[3,384,32,32]{1,3,2,0:T(8,128)(2,1)} %get-tuple-element.10, bf16[3,384,32,32]{1,3,2,0:T(8,128)(2,1)} %get-tuple-element.9, bf16[3,1536,64]{1,2,0:T(8,128)(2,1)S(1)} %all_gather.15), kind=kOutput, calls=%fused_computation.28 | convolution fusion | flops 7257194496 | bytes 231800832 | tf_op jit(solution)/shard_map/nshd,ntd->nhst/dot_general | solution.py:33
  233.1 37.9 %all-gather.5.cloned.1.call-done = bf16[3,1536,32,128]{3,1,2,0:T(8,128)(2,1)} async-done(((bf16[3,384,32,128]{3,1,2,0:T(8,128)(2,1)}), bf16[3,1536,32,128]{3,1,2,0:T(8,128)(2,1)}) %all-gather.5.cloned.1.call-update) | async-done | bytes 37748752 | tf_op jit(solution)/shard_map/all_gather | solution.py:66
  271.0 177.3 %fusion.40 = (f32[3,32,384]{2,1,0:T(8,128)S(1)}, f32[3,32,384,1536]{3,2,1,0:T(8,128)}) fusion(f32[3,1536,384,32]{1,2,3,0:T(8,128)} %fusion.20, pred[3,384,1536]{2,1,0:T(8,128)(4,1)S(1)} %broadcast_compare_fusion, bf16[3,1536,32,128]{3,1,2,0:T(8,128)(2,1)} %all-gather.5.cloned.1.call-done, bf16[3,384,32,192]{1,3,2,0:T(8,128)(2,1)} %bitcast.59), kind=kOutput, calls=%fused_computation.57 | convolution fusion | flops 14778631168 | bytes 502087680 | tf_op jit(solution)/shard_map/sub | solution.py:36
  448.4 51.3 %all-gather.3.cloned.1.call-done = bf16[3,1536,32,128]{1,3,2,0:T(8,128)(2,1)} async-done(((bf16[3,384,32,128]{1,3,2,0:T(8,128)(2,1)}), bf16[3,1536,32,128]{1,3,2,0:T(8,128)(2,1)}) %all-gather.3.cloned.1.call-update) | async-done | bytes 37748752 | tf_op jit(solution)/shard_map/all_gather | solution.py:67
  499.7 82.4 %fusion.17 = bf16[3,32,128,384]{3,2,1,0:T(8,128)(2,1)} fusion(bf16[3,1536,32,128]{1,3,2,0:T(8,128)(2,1)} %all-gather.3.cloned.1.call-done, f32[3,32,384,1536]{3,2,1,0:T(8,128)} %get-tuple-element.18, f32[3,32,384]{2,1,0:T(8,128)S(1)} %get-tuple-element.17), kind=kOutput, calls=%fused_computation.24 | convolution fusion | flops 14613479424 | bytes 273825792 | tf_op jit(solution)/shard_map/nhst,nthd->nshd/dot_general | solution.py:37
  582.0 58.5 %fusion.4 = f32[3,384,5120]{2,1,0:T(8,128)} fusion(bf16[3,384,4096]{1,2,0:T(8,128)(2,1)} %bitcast.62, bf16[4096,5120]{1,0:T(8,128)(2,1)} %param.19), kind=kOutput, calls=%fused_computation.7 | convolution fusion | flops 48318382080 | bytes 74973184 | tf_op jit(solution)/shard_map/nsk,kd->nsd/dot_general | solution.py:71
  640.6 1.2 copy-done.1
  641.8 1.4 copy.30
  643.3 776.5 %all-reduce.2.cloned.1.call-done = f32[3,384,5120]{2,1,0:T(8,128)} async-done(((f32[3,384,5120]{2,1,0:T(8,128)}), f32[3,384,5120]{2,1,0:T(8,128)}) %all-reduce.2.cloned.1.call-update) | async-done | bytes 23592976 | tf_op jit(solution)/shard_map/psum | solution.py:72
  1419.8 15.9 %add_convert_fusion = bf16[3,384,5120]{2,1,0:T(8,128)(2,1)} fusion(f32[3,384,5120]{2,1,0:T(8,128)} %all-reduce.2.cloned.1.call-done, bf16[3,384,5120]{2,1,0:T(8,128)(2,1)} %param.10), kind=kLoop, calls=%fused_computation.9 | loop fusion | flops 17694720 | bytes 47185920 | tf_op jit(solution)/shard_map/convert_element_type | solution.py:73
  (19 shorter events, 0.1 us)
Async XLA Ops:
  7.2 12.2 copy-start.4
  7.2 263.9 %all-gather.5.cloned.1.call-start = ((), (), s32[]{:S(2)}) async-start(), calls=%async_computation.1 | async-start | bytes 47185920 | tf_op jit(solution)/shard_map/all_gather | solution.py:66
  7.2 12.5 copy-start.5
  19.7 17.6 %copy-start = (bf16[3,384,512]{1,2,0:T(8,128)(2,1)}, bf16[3,384,512]{1,2,0:T(8,128)(2,1)S(1)}, u32[]{:S(2)}) copy-start(bf16[3,384,512]{1,2,0:T(8,128)(2,1)S(1)} %fusion.34) | copy-start | bytes 3538948
  37.3 462.4 %all-gather.3.cloned.1.call-start = ((), (), s32[]{:S(2)}) async-start(), calls=%async_computation | async-start | bytes 47185920 | tf_op jit(solution)/shard_map/all_gather | solution.py:67
  59.4 0.7 copy-start.3
  59.4 1360.3 %all-reduce.2.cloned.1.call-start = ((), (), s32[]{:S(2)}) async-start(), calls=%async_computation.2 | async-start | bytes 47185920 | tf_op jit(solution)/shard_map/psum | solution.py:72
  60.1 25.1 %copy-start.6 = (f32[1536]{0:T(1024)S(1)}, f32[1536]{0:T(1024)}, u32[]{:S(2)}) copy-start(f32[1536]{0:T(1024)} %param.13) | copy-start | bytes 18436
  138.7 18.5 %copy-start.2 = (bf16[3,384,64]{1,2,0:T(8,128)(2,1)}, bf16[3,384,64]{1,2,0:T(8,128)(2,1)S(1)}, u32[]{:S(2)}) copy-start(bf16[3,384,64]{1,2,0:T(8,128)(2,1)S(1)} %pad_maximum_fusion) | copy-start | bytes 442372
  640.6 1.3 copy-start.1
Sparse Core Ops, SparseCore 0:
  37.4 233.5 all-gather.4
  272.6 227.0 all-gather.2
  640.7 778.9 all-reduce.1
where the time goes:
time: 1450 us; the launch traced here: 1440 us
  waiting for transfers between devices  866 us (60%)
  matrix products  475 us (33%)
  local copies, waits for them, and re-layouts  44.4 us (3%)
  other arithmetic  25 us (2%)
  blocking collectives  18.2 us (1%)
    psum x1, waiting for transfers between devices, local_step(): head_sum = lax.psum(part_out, 'tp')  776 us
    sub x1, matrix products, attend(): probs_bf = jax.nn.softmax(scores, axis=-1).astype(jnp.bfloat16)  177 us
    dot_general x1, matrix products, attend(): jnp.einsum('nhst,nthd->nshd', probs_bf, values, preferred_element_type=jn...  82.4 us
    dot_general x1, matrix products, attend(): jnp.einsum('nshd,ntd->nhst', q_rope, k_rope, preferred_element_type=jnp.f...  74.9 us
    dot_general x1, matrix products, local_step(): jnp.einsum('nsk,kd->nsd', attn_out, w_o, preferred_element_type=jnp.float32)  58.5 us
    all_gather x1, waiting for transfers between devices, local_step(): values_all = lax.all_gather(values, 'cp', axis=1, tiled=True)  51.3 us
    all_gather x1, waiting for transfers between devices, local_step(): k_nope_all = lax.all_gather(k_nope, 'cp', axis=1, tiled=True)  37.9 us
  transfers between devices with their start and end apart: 3, of which 3 were waited for; matrix products, arithmetic and copies ran while one was open for 25% of the time, Pallas kernels for 0%

commit v1 on v0

v1 whole, which is shorter than its diff:
```python
import functools

import jax
import jax.numpy as jnp
from jax import lax
from jax.experimental import pallas as pl
from jax.experimental.pallas import tpu as pltpu
from jax.sharding import PartitionSpec as P


ROPE_BASE = 10000.0
NORM_EPS = 1e-6
LOG2_E = 1.4426950408889634
CHUNKS = 24
PAIR = 2
SPLITS = 3


def rms_norm(tensor, norm_gain):
    tensor_f32 = tensor.astype(jnp.float32)
    inv_rms = lax.rsqrt(jnp.mean(tensor_f32 * tensor_f32, axis=-1, keepdims=True) + NORM_EPS)
    return (tensor_f32 * inv_rms * norm_gain).astype(jnp.bfloat16)


def rope_tables(positions, rope_dim):
    inv_freq = ROPE_BASE ** (-2.0 * jnp.arange(rope_dim // 2, dtype=jnp.float32) / rope_dim)
    angles = positions.astype(jnp.float32)[..., None] * inv_freq
    return jnp.cos(angles), jnp.sin(angles)


def rotate(tensor, cos_t, sin_t):
    tensor_f32 = tensor.astype(jnp.float32)
    half_dim = tensor_f32.shape[-1] // 2
    lower_half = tensor_f32[..., :half_dim]
    upper_half = tensor_f32[..., half_dim:]
    return jnp.concatenate([lower_half * cos_t - upper_half * sin_t,
                            lower_half * sin_t + upper_half * cos_t], axis=-1).astype(jnp.bfloat16)


def attend_kernel(soft_scale, order_ref, q_ref, cos_ref, sin_ref, lat_hbm, w_uk_ref, w_uv_ref, *rest):
    o_ref, lat_s, sems = rest[-3:]
    n_blocks, block_len, _ = lat_hbm.shape
    half_keys = n_blocks // 2 * block_len
    rank = w_uk_ref.shape[0]
    rope_dim = cos_ref.shape[1]
    nope_dim = w_uk_ref.shape[1] // PAIR
    v_dim = w_uv_ref.shape[1] // PAIR
    qk_dim = nope_dim + rope_dim

    @pl.when(pl.program_id(0) == 0)
    def _():
        copies = [pltpu.make_async_copy(lat_hbm.at[order_ref[j]], lat_s.at[pl.ds(j * block_len, block_len)], sems.at[j])
                  for j in range(n_blocks)]
        for copy in copies:
            copy.start()
        for copy in copies:
            copy.wait()

    low_id = order_ref[n_blocks]
    latent = lat_s[:, :rank]
    k_rope = lat_s[:, rank:rank + rope_dim]
    k_pair = jnp.dot(latent, w_uk_ref[...], preferred_element_type=jnp.float32).astype(jnp.bfloat16)
    v_pair = jnp.dot(latent, w_uv_ref[...], preferred_element_type=jnp.float32).astype(jnp.bfloat16)

    q_pair = q_ref[...].astype(jnp.float32)
    cos2 = cos_ref[...]
    sin2 = sin_ref[...]
    col_minus_row = (lax.broadcasted_iota(jnp.int32, (block_len, half_keys), 1)
                     - lax.broadcasted_iota(jnp.int32, (block_len, half_keys), 0))
    low_mask = col_minus_row <= low_id * block_len
    high_mask = col_minus_row <= (n_blocks - 1 - low_id) * block_len - half_keys
    factor = soft_scale * LOG2_E
    contract_last = (((1,), (1,)), ((), ()))

    for head in range(PAIR):
        q_head = q_pair if head == 0 else pltpu.roll(q_pair, (PAIR - head) * qk_dim, 1)
        q_rope = q_head[:, nope_dim:qk_dim]
        swapped = jnp.concatenate([q_rope[:, rope_dim // 2:], q_rope[:, :rope_dim // 2]], axis=1)
        q_rot = q_rope * cos2 + swapped * sin2
        q_cat = jnp.concatenate([q_head[:, :nope_dim], q_rot], axis=1).astype(jnp.bfloat16)
        k_cat = jnp.concatenate([k_pair[:, head * nope_dim:(head + 1) * nope_dim], k_rope], axis=1)
        v_head = v_pair[:, head * v_dim:(head + 1) * v_dim]
        early = lax.dot_general(q_cat, k_cat[:half_keys], contract_last, preferred_element_type=jnp.float32)
        late = lax.dot_general(q_cat[block_len:], k_cat[half_keys:], contract_last,
                               preferred_element_type=jnp.float32)

        low = jnp.where(low_mask, early[:block_len], -jnp.inf)
        low_exp = jnp.exp2((low - jnp.max(low, axis=1, keepdims=True)) * factor)
        low_prob = (low_exp * (1.0 / jnp.sum(low_exp, axis=1, keepdims=True))).astype(jnp.bfloat16)
        low_out = jnp.dot(low_prob, v_head[:half_keys], preferred_element_type=jnp.float32)

        near = early[block_len:]
        far = jnp.where(high_mask, late, -jnp.inf)
        top = jnp.maximum(jnp.max(near, axis=1, keepdims=True), jnp.max(far, axis=1, keepdims=True))
        near_exp = jnp.exp2((near - top) * factor)
        far_exp = jnp.exp2((far - top) * factor)
        inv_sum = 1.0 / (jnp.sum(near_exp, axis=1, keepdims=True) + jnp.sum(far_exp, axis=1, keepdims=True))
        high_out = (jnp.dot((near_exp * inv_sum).astype(jnp.bfloat16), v_head[:half_keys],
                            preferred_element_type=jnp.float32)
                    + jnp.dot((far_exp * inv_sum).astype(jnp.bfloat16), v_head[half_keys:],
                              preferred_element_type=jnp.float32))
        o_ref[:block_len, head * v_dim:(head + 1) * v_dim] = low_out.astype(jnp.bfloat16)
        o_ref[block_len:, head * v_dim:(head + 1) * v_dim] = high_out.astype(jnp.bfloat16)


def attend(q_full, cos2, sin2, lat_blocks, order, w_uk, w_uv, heads, soft_scale, pairs, prior):
    n_blocks, block_len, width = lat_blocks.shape
    tokens = q_full.shape[0]
    rank = w_uk.shape[0]
    keys = n_blocks * block_len
    qk_dim = q_full.shape[1] // heads
    nope_dim = w_uk.shape[1] // heads
    v_dim = w_uv.shape[1] // heads
    rope_dim = cos2.shape[1]
    first, count = pairs[0], len(pairs)
    flops = (2 * keys * rank * (nope_dim + v_dim) + 2 * tokens * keys * 3 // 4 * (qk_dim + v_dim)) * count * PAIR
    moved = 2 * (lat_blocks.size + (tokens * (qk_dim + v_dim) + rank * (nope_dim + v_dim)) * count * PAIR)
    in_specs = [
        pl.BlockSpec((tokens, PAIR * qk_dim), lambda h, order: (0, h + first)),
        pl.BlockSpec((tokens, rope_dim), lambda h, order: (0, 0)),
        pl.BlockSpec((tokens, rope_dim), lambda h, order: (0, 0)),
        pl.BlockSpec(memory_space=pl.ANY),
        pl.BlockSpec((rank, PAIR * nope_dim), lambda h, order: (0, h + first)),
        pl.BlockSpec((rank, PAIR * v_dim), lambda h, order: (0, h + first)),
    ]
    operands = [q_full, cos2, sin2, lat_blocks, w_uk, w_uv]
    aliases = {}
    if prior is not None:
        in_specs.append(pl.BlockSpec(memory_space=pl.ANY))
        operands.append(prior)
        aliases = {len(operands): 0}
    return pl.pallas_call(
        functools.partial(attend_kernel, soft_scale),
        out_shape=jax.ShapeDtypeStruct((tokens, heads * v_dim), jnp.bfloat16),
        grid_spec=pltpu.PrefetchScalarGridSpec(
            num_scalar_prefetch=1,
            grid=(count,),
            in_specs=in_specs,
            out_specs=pl.BlockSpec((tokens, PAIR * v_dim), lambda h, order: (0, h + first)),
            scratch_shapes=[pltpu.VMEM((keys, width), jnp.bfloat16), pltpu.SemaphoreType.DMA((n_blocks,))],
        ),
        input_output_aliases=aliases,
        compiler_params=pltpu.CompilerParams(dimension_semantics=("arbitrary",), vmem_limit_bytes=56 * 1024 * 1024),
        cost_estimate=pl.CostEstimate(flops=flops, bytes_accessed=moved,
                                      transcendentals=tokens * keys * count * PAIR * 3 // 4),
        name="attend",
    )(order, *operands)


def together(*values):
    return lax.optimization_barrier(values)


def chain_sum(partials, pieces, x_rows, n_tp, chunks):
    num_seq = pieces.num_seq
    rows, width = x_rows.shape
    size = rows // chunks
    half = width // 2
    per = chunks // num_seq
    last = n_tp - 1
    z = lax.axis_index('tp')
    z_rows = z * size
    out = jnp.zeros((rows, width), jnp.bfloat16)

    def part(step, index, which):
        lo, hi = max(step - last, 0) // per, min(step, chunks - 1) // per
        pick = None
        for n in range(lo, hi + 1):
            at = index - n * per * size
            piece = lax.dynamic_slice(partials[n][which], (at, 0), (size, half), allow_negative_indices=False)
            pick = piece if pick is None else jnp.where(at >= 0, piece, pick)
        return pick

    def send(value, step, up, live):
        pairs = []
        for d in range(n_tp):
            to = d + 1 if up else d - 1
            if 0 <= to < n_tp and 0 <= live(d, step) < chunks:
                pairs.append((d, to))
        if not pairs:
            return None
        return lax.ppermute(value, 'tp', pairs)

    sum_up = sum_dn = None
    got_b = got_a = None
    fin_b = fin_a = None
    keep_b = keep_a = None
    for t in range(chunks + 2 * last + 1):
        moving = t < chunks + last
        returning = 0 <= t - 1 - last and t - 1 - 2 * last < chunks
        up = dn = val_b = val_a = None
        if returning:
            base_b = t - 1 - 2 * last
            base_a = t - 1 - last
            val_b = fin_b if got_b is None else (got_b if fin_b is None else jnp.where(z == last, fin_b, got_b))
            val_a = fin_a if got_a is None else (got_a if fin_a is None else jnp.where(z == 0, fin_a, got_a))
        if moving:
            up = part(t, t * size - z_rows, 1)
            dn = part(t, (t - last) * size + z_rows, 0)
            if sum_up is not None:
                up = up + jnp.where(z == 0, 0.0, sum_up)
                dn = dn + jnp.where(z == last, 0.0, sum_dn)
        gates = [v for v in (up, dn, val_b, val_a) if v is not None]
        if moving:
            gates.append(x_rows)
            gates = list(pieces.open(gates) if pieces.left() else together(*gates))
            x_rows = gates.pop()
        if moving:
            up, dn = gates[:2]
            gates = gates[2:]
        if returning:
            val_b, val_a = gates
        next_up = next_dn = next_b = next_a = None
        if moving:
            next_up = send(up, t, True, lambda d, s: s - d)
            next_dn = send(dn, t, False, lambda d, s: s - last + d)
        if returning:
            next_b = send(val_b, t, False, lambda d, s: s - 1 - 2 * last + d)
            next_a = send(val_a, t, True, lambda d, s: s - 1 - last - d)
            idx_b = base_b * size + z_rows
            idx_a = base_a * size - z_rows
            if t - 1 - last >= chunks:
                val_b = jnp.where(idx_b < rows, val_b, keep_b)
                val_a = jnp.where(idx_a < rows, val_a, keep_a)
            keep_b, keep_a = val_b, val_a
            out = lax.dynamic_update_slice(out, val_b, (idx_b, half), allow_negative_indices=False)
            out = lax.dynamic_update_slice(out, val_a, (idx_a, 0), allow_negative_indices=False)
        fin_b = fin_a = None
        if moving and t >= last:
            x_piece = lax.slice(x_rows, ((t - last) * size, 0), ((t - last + 1) * size, width)).astype(jnp.float32)
            fin_b = (x_piece[:, half:] + up).astype(jnp.bfloat16)
            fin_a = (x_piece[:, :half] + dn).astype(jnp.bfloat16)
        if pieces.left():
            done = [v for v in (next_up, next_dn, next_b, next_a) if v is not None]
            done = iter(pieces.close(done))
            next_up, next_dn, next_b, next_a = [None if v is None else next(done)
                                                for v in (next_up, next_dn, next_b, next_a)]
        sum_up, sum_dn, got_b, got_a = next_up, next_dn, next_b, next_a
    return out


class Pieces:
    def __init__(self, steps, first, num_seq):
        self.steps = list(steps)
        self.state = first
        self.num_seq = num_seq
        self.at = 0

    def left(self):
        return self.at < len(self.steps)

    def open(self, gates):
        tied = together(*self.state, *gates)
        count = len(self.state)
        self.state = tuple(self.steps[self.at](*tied[:count]))
        return tied[count:]

    def close(self, done):
        tied = together(*self.state, *done)
        self.state = tuple(tied[:len(self.state)])
        self.at += 1
        return tied[len(self.state):]


def solution(mesh):
    n_tp = mesh.shape['tp']
    n_cp = mesh.shape['cp']

    def local_block(x_blk, pos_blk, w_dq, g_q, w_uq, w_dkv, g_kv, w_uk, w_uv, w_o):
        num_seq, seq_dev, width = x_blk.shape
        kv_rank = g_kv.shape[0]
        rope_dim = w_dkv.shape[1] - kv_rank
        heads_dev = (w_uq.shape[1] - w_uk.shape[1]) // rope_dim
        nope_dim = w_uk.shape[1] // heads_dev
        soft_scale = (nope_dim + rope_dim) ** -0.5
        n_blocks = 2 * n_cp
        block_len = seq_dev // 2
        n_pairs = heads_dev // PAIR
        cuts = [n_pairs * i // SPLITS for i in range(SPLITS + 1)]
        pos_f32 = pos_blk.astype(jnp.float32)
        x_flat = x_blk.reshape(num_seq * seq_dev, width)
        latents, ropes, tables, gathered, orders = {}, {}, {}, {}, {}
        partials = []

        def compress(rows, pos_rows, prompts):
            cos_t, sin_t = rope_tables(pos_rows, rope_dim)
            kv_joint = jnp.dot(rows, w_dkv, preferred_element_type=jnp.float32).astype(jnp.bfloat16)
            latent = rms_norm(kv_joint[:, :kv_rank], g_kv)
            k_rope = rotate(kv_joint[:, kv_rank:], cos_t, sin_t)
            block_ids = jnp.broadcast_to(jnp.floor(pos_rows / block_len)[:, None].astype(jnp.bfloat16), k_rope.shape)
            both = jnp.concatenate([latent, k_rope, block_ids], axis=1)
            both = both.reshape(len(prompts), seq_dev, -1)
            both_all = lax.all_gather(both, 'cp', axis=1, tiled=True)
            cos2 = jnp.concatenate([cos_t, cos_t], axis=1).reshape(len(prompts), seq_dev, rope_dim)
            sin2 = jnp.concatenate([-sin_t, sin_t], axis=1).reshape(len(prompts), seq_dev, rope_dim)
            for i, n in enumerate(prompts):
                latents[n] = latent[i * seq_dev:(i + 1) * seq_dev]
                ropes[n] = k_rope[i * seq_dev:(i + 1) * seq_dev]
                tables[n] = (cos2[i], sin2[i])
                gathered[n] = both_all[i].reshape(n_blocks, block_len, -1)

        def order_of(n):
            ids_all = gathered[n][:, 0, kv_rank + rope_dim].astype(jnp.int32)
            blocks = jnp.arange(n_blocks, dtype=jnp.int32)
            where = jnp.sum(jnp.where(ids_all[None, :] == blocks[:, None], blocks[None, :], 0), axis=1)
            return jnp.concatenate([where, pos_blk[n, :1] // block_len]).astype(jnp.int32)

        def q_down(rows):
            return jnp.dot(rows, w_dq, preferred_element_type=jnp.float32).astype(jnp.bfloat16)

        def q_up(q_latent):
            return jnp.dot(rms_norm(q_latent, g_q), w_uq, preferred_element_type=jnp.float32).astype(jnp.bfloat16)

        def heads_of(n, q_full, pairs, prior):
            return attend(q_full, *tables[n], gathered[n], orders[n], w_uk, w_uv, heads_dev, soft_scale, pairs, prior)

        def product(attn, which):
            cols = w_o.shape[1] // 2
            return jnp.dot(attn, w_o[:, which * cols:(which + 1) * cols], preferred_element_type=jnp.float32)

        def later(n):
            rows = slice(n * seq_dev, (n + 1) * seq_dev)

            def step_down(x_all):
                return x_all, q_down(x_all[rows])

            def step_up(x_all, q_latent):
                if n not in orders:
                    orders[n] = order_of(n)
                return x_all, q_up(q_latent)

            def step_attend(i, x_all, q_full, *prior):
                attn = heads_of(n, q_full, range(cuts[i], cuts[i + 1]), prior[0] if prior else None)
                return (x_all, q_full, attn) if i + 1 < SPLITS else (x_all, attn)

            def step_second(x_all, attn):
                return x_all, attn, product(attn, 1)

            def step_first(x_all, attn, second):
                partials.append((product(attn, 0), second))
                return x_all, *partials[-1]

            def step_settle(x_all, first, second):
                partials[n] = (first, second)
                return (x_all,)

            return ([step_down, step_up] + [functools.partial(step_attend, i) for i in range(SPLITS)]
                    + [step_second, step_first], step_settle)

        compress(x_flat[:seq_dev], pos_f32[0], [0])
        q_full = q_up(q_down(x_flat[:seq_dev]))
        orders[0] = order_of(0)
        attn = heads_of(0, q_full, range(n_pairs), None)
        partials.append((product(attn, 0), product(attn, 1)))

        def step_compress(x_all):
            rest = list(range(1, num_seq))
            compress(x_all[seq_dev:], pos_f32[1:].reshape(-1), rest)
            return x_all, jnp.concatenate([latents[n] for n in rest])

        steps = [step_compress]
        first_state = (x_flat,)
        chain = []
        for n in range(1, num_seq):
            work, settle = later(n)
            chain.append((work, settle))
        steps = [step_compress]
        pending = lambda x_all, *_: (x_all,)
        for work, settle in chain:
            head = functools.partial(lambda before, fn, *state: fn(*before(*state)), pending, work[0])
            steps += [head] + work[1:]
            pending = settle
        pieces = Pieces(steps, first_state, num_seq)
        out = chain_sum(partials, pieces, x_flat, n_tp, CHUNKS)
        out = out.reshape(x_blk.shape)
        return (out, jnp.stack([latents[n] for n in range(num_seq)]), jnp.stack([ropes[n] for n in range(num_seq)]))

    seq_spec = P('dp', 'cp', None)
    in_specs = (seq_spec, P('dp', 'cp'), P(None, None), P(None), P(None, 'tp'), P(None, None), P(None),
                P(None, 'tp'), P(None, 'tp'), P('tp', None))
    return jax.shard_map(local_block, mesh=mesh, in_specs=in_specs,
                         out_specs=(seq_spec, seq_spec, seq_spec), check_vma=False)
```

time: 1450 us -> 924 us (0.64)
  waiting for transfers between devices: 866 us -> 127 us
  matrix products: 475 us -> 175 us
  starting transfers between devices: 0.29 us -> 290 us
  Pallas kernels: 0 us -> 172 us
  other arithmetic: 25 us -> 75.8 us
  blocking collectives: 18.2 us -> 0 us
    psum x1 -> x0, waiting for transfers between devices: 776 us -> none  [local_step(): head_sum = lax.psum(part_out, 'tp')]
    ppermute x0 -> x104, starting transfers between devices: none -> 290 us  [send(): return lax.ppermute(value, 'tp', pairs)]
    sub x1 -> x0, matrix products: 177 us -> none  [attend(): probs_bf = jax.nn.softmax(scores, axis=-1).astype(jnp.bfloat16)]
    pallas_call x0 -> x7, Pallas kernels: none -> 172 us  [attend(): pl.pallas_call(functools.partial(attend_kernel, soft_scale), out_shape=ja...]
    ppermute x0 -> x104, waiting for transfers between devices: none -> 127 us  [send(): return lax.ppermute(value, 'tp', pairs)]
    dot_general x8 -> x14, matrix products: 297 us -> 175 us  [the longest x6 85.2 us: product(): jnp.dot(attn, w_o[:, which * cols:(which + 1) * cols], preferred_element_...]
    all_gather x2, waiting for transfers between devices: 89.2 us -> 0.02 us  [compress(): both_all = lax.all_gather(both, 'cp', axis=1, tiled=True)]
    add x0 -> x51, other arithmetic: none -> 38.4 us  [the longest x26 21.7 us: chain_sum(): dn = dn + jnp.where(z == last, 0.0, sum_dn)]
  transfers between devices with their start and end apart: 3 -> 106, of which waited for: 3 -> 31; matrix products, arithmetic and copies ran while one was open for 25% -> 14% of each run, Pallas kernels for 0% -> 13%
where the time goes in v1:
time: 924 us; the launch traced here: 914 us
  starting transfers between devices  290 us (31%)
  matrix products  175 us (19%)
  Pallas kernels  172 us (19%)
  waiting for transfers between devices  127 us (14%)
  other arithmetic  75.8 us (8%)
  local copies, waits for them, and re-layouts  52.1 us (6%)
  between operations  22.5 us (2%)
    ppermute x104, starting transfers between devices, send(): return lax.ppermute(value, 'tp', pairs)  290 us
    pallas_call x7, Pallas kernels, attend(): pl.pallas_call(functools.partial(attend_kernel, soft_scale), out_shape=ja...  172 us
    ppermute x104, waiting for transfers between devices, send(): return lax.ppermute(value, 'tp', pairs)  127 us
    dot_general x6, matrix products, product(): jnp.dot(attn, w_o[:, which * cols:(which + 1) * cols], preferred_element_...  85.2 us
    dot_general x3, matrix products, q_up(): jnp.dot(rms_norm(q_latent, g_q), w_uq, preferred_element_type=jnp.float32)  40.8 us
    dot_general x3, matrix products, q_down(): jnp.dot(rows, w_dq, preferred_element_type=jnp.float32).astype(jnp.bfloat16)  32.9 us
    add x26, other arithmetic, chain_sum(): dn = dn + jnp.where(z == last, 0.0, sum_dn)  21.7 us
  transfers between devices with their start and end apart: 106, of which 31 were waited for; matrix products, arithmetic and copies ran while one was open for 14% of the time, Pallas kernels for 13%

profile of v1, /device:TPU:0, one launch (start us, length us, event | category | flops | bytes accessed | tf_op | source)
XLA Modules:
  0.0 914.0 jit_solution(10504646397643434476)
XLA Ops:
  7.2 7.1 fusion.48
  24.5 11.8 %fusion.33 = (f32[384]{0:T(512)S(1)}, bf16[384,1536]{1,0:T(8,128)(2,1)S(1)}) fusion(bf16[5120,1536]{1,0:T(8,128)(2,1)} %param.12, bf16[3,384,5120]{2,1,0:T(8,128)(2,1)} %param.10), kind=kOutput, calls=%fused_computation.36 | convolution fusion | flops 6042156544 | bytes 20841984 | tf_op jit(solution)/shard_map/dot_general | solution.py:309
  38.1 15.8 %convolution_convert_fusion.2.q_ref = bf16[384,6144]{1,0:T(8,128)(2,1)} fusion(bf16[1536,6144]{1,0:T(8,128)(2,1)} %param.14, bf16[384,1536]{1,0:T(8,128)(2,1)S(1)} %get-tuple-element.569, f32[1536]{0:T(1024)S(1)} %copy-done.26, f32[384]{0:T(512)S(1)} %add_rsqrt_fusion.3), kind=kOutput, calls=%fused_computation.14 | convolution fusion | flops 7252475904 | bytes 24780288 | tf_op jit(solution)/shard_map/dot_general | solution.py:312
  55.7 51.4 %attend.7 = bf16[384,4096]{1,0:T(8,128)(2,1)} custom-call(s32[9]{0:T(128)} %pad_add_fusion.order_ref, bf16[384,6144]{1,0:T(8,128)(2,1)} %convolution_convert_fusion.2.q_ref, f32[384,64]{1,0:T(8,128)} %pad_maximum_fusion.6.cos_ref, f32[384,64]{1,0:T(8,128)} %pad_maximum_fusion.7.sin_ref, bf16[8,192,640]{2,1,0:T(8,128)(2,1)} %bitcast.95, ...), custom_call_target="tpu_custom_call" | custom-call | flops 21944598528 | bytes 18219008 | tf_op jit(solution)/shard_map/attend/pallas_call | solution.py:132
  107.1 14.8 %fusion.4 = f32[384,2560]{1,0:T(8,128)} fusion(bf16[384,4096]{1,0:T(8,128)(2,1)} %attend.7, bf16[4096,5120]{1,0:T(8,128)(2,1)} %param.19), kind=kOutput, calls=%fused_computation.4 | convolution fusion | flops 8053063680 | bytes 28049408 | tf_op jit(solution)/shard_map/dot_general | solution.py:319
  121.9 13.7 %fusion.10 = f32[384,2560]{1,0:T(8,128)S(1)} fusion(bf16[384,4096]{1,0:T(8,128)(2,1)} %attend.7, bf16[4096,5120]{1,0:T(8,128)(2,1)} %param.19), kind=kOutput, calls=%fused_computation.10 | convolution fusion | flops 8053063680 | bytes 28049408 | tf_op jit(solution)/shard_map/dot_general | solution.py:319
  138.7 9.0 fusion.45
  170.8 11.2 %fusion.24 = bf16[384,1536]{1,0:T(8,128)(2,1)S(1)} fusion(bf16[5120,1536]{1,0:T(8,128)(2,1)} %param.12, bf16[1152,5120]{1,0:T(8,128)(2,1)} %bitcast.49), kind=kOutput, calls=%fused_computation.33 | convolution fusion | flops 6040387584 | bytes 20840448 | tf_op jit(solution)/shard_map/dot_general | solution.py:309
  184.6 6.1 collective-permute-start.4
  192.1 9.2 %convolution_convert_fusion.1.q_ref = bf16[384,6144]{1,0:T(8,128)(2,1)} fusion(bf16[1536,6144]{1,0:T(8,128)(2,1)S(1)} %bitcast.97, bf16[384,1536]{1,0:T(8,128)(2,1)S(1)} %fusion.24, f32[384]{0:T(512)S(1)} %add_rsqrt_fusion.2, f32[1536]{0:T(1024)S(1)} %copy-done.26), kind=kOutput, calls=%fused_computation.13 | convolution fusion | flops 7252475904 | bytes 24780288 | tf_op jit(solution)/shard_map/dot_general | solution.py:312
  217.1 19.0 %attend.8.rest_0_ = bf16[384,4096]{1,0:T(8,128)(2,1)} custom-call(s32[9]{0:T(128)} %pad_add_fusion.1.order_ref, bf16[384,6144]{1,0:T(8,128)(2,1)} %convolution_convert_fusion.1.q_ref, f32[384,64]{1,0:T(8,128)} %get-tuple-element.574.cos_ref, f32[384,64]{1,0:T(8,128)} %get-tuple-element.546.sin_ref, bf16[8,192,640]{2,1,0:T(8,128)(2,1)} %bitcast.89, ...), custom_call_target="tpu_custom_call" | custom-call | flops 6857687040 | bytes 7045120 | tf_op jit(solution)/shard_map/attend/pallas_call | solution.py:132
  250.6 6.0 broadcast_in_dim.115
  257.3 19.1 %attend.9.rest_0_ = bf16[384,4096]{1,0:T(8,128)(2,1)} custom-call(s32[9]{0:T(128)} %pad_add_fusion.1.order_ref, bf16[384,6144]{1,0:T(8,128)(2,1)} %convolution_convert_fusion.1.q_ref, f32[384,64]{1,0:T(8,128)} %get-tuple-element.574.cos_ref, f32[384,64]{1,0:T(8,128)} %get-tuple-element.546.sin_ref, ...), custom_call_target="tpu_custom_call", output_to_operand_aliasing={{}: (7, {})} | custom-call | flops 6857687040 | bytes 7045120 | tf_op jit(solution)/shard_map/attend/pallas_call | solution.py:132
  289.8 21.9 %attend.10 = bf16[384,4096]{1,0:T(8,128)(2,1)} custom-call(s32[9]{0:T(128)} %pad_add_fusion.1.order_ref, bf16[384,6144]{1,0:T(8,128)(2,1)} %convolution_convert_fusion.1.q_ref, f32[384,64]{1,0:T(8,128)} %get-tuple-element.574.cos_ref, f32[384,64]{1,0:T(8,128)} %get-tuple-element.546.sin_ref, ...), custom_call_target="tpu_custom_call", output_to_operand_aliasing={{}: (7, {})} | custom-call | flops 8229224448 | bytes 8060928 | tf_op jit(solution)/shard_map/attend/pallas_call | solution.py:132
  315.9 13.6 %fusion.8 = f32[384,2560]{1,0:T(8,128)S(1)} fusion(bf16[384,4096]{1,0:T(8,128)(2,1)} %attend.10, bf16[4096,5120]{1,0:T(8,128)(2,1)} %param.19), kind=kOutput, calls=%fused_computation.8 | convolution fusion | flops 8053063680 | bytes 28049408 | tf_op jit(solution)/shard_map/dot_general | solution.py:319
  352.3 14.9 %fusion.2 = f32[384,2560]{1,0:T(8,128)} fusion(bf16[384,4096]{1,0:T(8,128)(2,1)} %attend.10, bf16[4096,5120]{1,0:T(8,128)(2,1)} %param.19), kind=kOutput, calls=%fused_computation.2 | convolution fusion | flops 8053063680 | bytes 28049408 | tf_op jit(solution)/shard_map/dot_general | solution.py:319
  386.9 9.9 %fusion.27 = bf16[384,1536]{1,0:T(8,128)(2,1)S(1)} fusion(bf16[5120,1536]{1,0:T(8,128)(2,1)} %param.12, bf16[1152,5120]{1,0:T(8,128)(2,1)S(1)} %bitcast.62), kind=kOutput, calls=%fused_computation.34 | convolution fusion | flops 6040387584 | bytes 20840448 | tf_op jit(solution)/shard_map/dot_general | solution.py:309
  417.4 15.8 %convolution_convert_fusion.q_ref = bf16[384,6144]{1,0:T(8,128)(2,1)} fusion(bf16[1536,6144]{1,0:T(8,128)(2,1)} %param.14, bf16[384,1536]{1,0:T(8,128)(2,1)S(1)} %fusion.27, f32[384]{0:T(512)S(1)} %add_rsqrt_fusion.1, f32[1536]{0:T(1024)S(1)} %copy-done.26), kind=kOutput, calls=%fused_computation.12 | convolution fusion | flops 7252475904 | bytes 24780288 | tf_op jit(solution)/shard_map/dot_general | solution.py:312
  460.8 5.9 collective-permute-start.35
  466.8 19.4 %attend.11.rest_0_ = bf16[384,4096]{1,0:T(8,128)(2,1)} custom-call(s32[9]{0:T(128)} %pad_add_fusion.2.order_ref, bf16[384,6144]{1,0:T(8,128)(2,1)} %convolution_convert_fusion.q_ref, f32[384,64]{1,0:T(8,128)} %get-tuple-element.575.cos_ref, f32[384,64]{1,0:T(8,128)} %get-tuple-element.545.sin_ref, bf16[8,192,640]{2,1,0:T(8,128)(2,1)} %bitcast.85, ...), custom_call_target="tpu_custom_call" | custom-call | flops 6857687040 | bytes 7045120 | tf_op jit(solution)/shard_map/attend/pallas_call | solution.py:132
  505.6 19.0 %attend.12.rest_0_ = bf16[384,4096]{1,0:T(8,128)(2,1)} custom-call(s32[9]{0:T(128)} %pad_add_fusion.2.order_ref, bf16[384,6144]{1,0:T(8,128)(2,1)} %convolution_convert_fusion.q_ref, f32[384,64]{1,0:T(8,128)} %get-tuple-element.575.cos_ref, f32[384,64]{1,0:T(8,128)} %get-tuple-element.545.sin_ref, ...), custom_call_target="tpu_custom_call", output_to_operand_aliasing={{}: (7, {})} | custom-call | flops 6857687040 | bytes 7045120 | tf_op jit(solution)/shard_map/attend/pallas_call | solution.py:132
  542.0 22.1 %attend.13 = bf16[384,4096]{1,0:T(8,128)(2,1)} custom-call(s32[9]{0:T(128)} %pad_add_fusion.2.order_ref, bf16[384,6144]{1,0:T(8,128)(2,1)} %convolution_convert_fusion.q_ref, f32[384,64]{1,0:T(8,128)} %get-tuple-element.575.cos_ref, f32[384,64]{1,0:T(8,128)} %get-tuple-element.545.sin_ref, ...), custom_call_target="tpu_custom_call", output_to_operand_aliasing={{}: (7, {})} | custom-call | flops 8229224448 | bytes 8060928 | tf_op jit(solution)/shard_map/attend/pallas_call | solution.py:132
  568.9 13.5 %fusion.6 = f32[384,2560]{1,0:T(8,128)S(1)} fusion(bf16[384,4096]{1,0:T(8,128)(2,1)} %attend.13, bf16[4096,5120]{1,0:T(8,128)(2,1)} %param.19), kind=kOutput, calls=%fused_computation.6 | convolution fusion | flops 8053063680 | bytes 28049408 | tf_op jit(solution)/shard_map/dot_general | solution.py:319
  603.0 14.7 %fusion = f32[384,2560]{1,0:T(8,128)} fusion(bf16[384,4096]{1,0:T(8,128)(2,1)} %attend.13, bf16[4096,5120]{1,0:T(8,128)(2,1)} %param.19), kind=kOutput, calls=%fused_computation | convolution fusion | flops 8053063680 | bytes 28049408 | tf_op jit(solution)/shard_map/dot_general | solution.py:319
  629.8 7.0 collective-permute-done.50
  653.1 6.0 collective-permute-done.53
  675.5 7.0 collective-permute-done.57
  699.5 8.4 collective-permute-done.61
  724.1 5.9 collective-permute-done.65
  834.9 5.9 collective-permute-start.91
  844.6 8.9 collective-permute-done.89
  863.4 6.9 collective-permute-done.93
  (489 shorter events, 470.6 us)
Async XLA Ops:
  7.2 46.8 %all-gather.6.cloned.1.call-start = ((), (), s32[]{:S(2)}) async-start(), calls=%async_computation.1 | async-start | bytes 2457600 | tf_op jit(solution)/shard_map/all_gather | solution.py:293
  17.1 195.1 %all-gather.4.cloned.1.call-start = ((), (), s32[]{:S(2)}) async-start(), calls=%async_computation | async-start | bytes 4915200 | tf_op jit(solution)/shard_map/all_gather | solution.py:293
  165.3 16.8 %collective-permute-start.2 = (f32[48,2560]{1,0:T(8,128)S(1)}, f32[48,2560]{1,0:T(8,128)S(1)}, u32[]{:S(2)}, u32[]{:S(2)}) collective-permute-start(f32[48,2560]{1,0:T(8,128)S(1)} %get-tuple-element.247), channel_id=1, source_target_pairs={{0,4},{4,8},{1,5},{5,9},{2,6},{6,10},{3,7},{7,11},{16,20},{20,24},... | collective-permute-start | bytes 1474568 | tf_op jit(solution)/shard_map/ppermute | solution.py:182
  184.6 16.7 %collective-permute-start.4 = (f32[48,2560]{1,0:T(8,128)S(1)}, f32[48,2560]{1,0:T(8,128)S(1)}, u32[]{:S(2)}, u32[]{:S(2)}) collective-permute-start(f32[48,2560]{1,0:T(8,128)S(1)} %select_add_fusion.49), channel_id=1, source_target_pairs={{0,4},{4,8},{8,12},{1,5},{5,9},{9,13},{2,6},{6,10},{10,14},{3,7},{... | collective-permute-start | bytes 1474568 | tf_op jit(solution)/shard_map/ppermute | solution.py:182
  206.0 30.1 %collective-permute-start.6 = (f32[48,2560]{1,0:T(8,128)S(1)}, f32[48,2560]{1,0:T(8,128)S(1)}, u32[]{:S(2)}, u32[]{:S(2)}) collective-permute-start(f32[48,2560]{1,0:T(8,128)S(1)} %select_add_fusion.47), channel_id=1, source_target_pairs={{0,4},{4,8},{8,12},{1,5},{5,9},{9,13},{2,6},{6,10},{10,14},{3,7},{... | collective-permute-start | bytes 1474568 | tf_op jit(solution)/shard_map/ppermute | solution.py:182
  209.6 26.5 %collective-permute-start.7 = (f32[48,2560]{1,0:T(8,128)S(1)}, f32[48,2560]{1,0:T(8,128)S(1)}, u32[]{:S(2)}, u32[]{:S(2)}) collective-permute-start(f32[48,2560]{1,0:T(8,128)S(1)} %select_add_fusion.46), channel_id=1, source_target_pairs={{4,0},{8,4},{12,8},{5,1},{9,5},{13,9},{6,2},{10,6},{14,10},{7,3},{... | collective-permute-start | bytes 1474568 | tf_op jit(solution)/shard_map/ppermute | solution.py:182
  238.3 39.6 %collective-permute-start.8 = (f32[48,2560]{1,0:T(8,128)S(1)}, f32[48,2560]{1,0:T(8,128)S(1)}, u32[]{:S(2)}, u32[]{:S(2)}) collective-permute-start(f32[48,2560]{1,0:T(8,128)S(1)} %select_add_fusion.45), channel_id=1, source_target_pairs={{0,4},{4,8},{8,12},{1,5},{5,9},{9,13},{2,6},{6,10},{10,14},{3,7},{... | collective-permute-start | bytes 1474568 | tf_op jit(solution)/shard_map/ppermute | solution.py:182
  242.9 35.0 %collective-permute-start.9 = (f32[48,2560]{1,0:T(8,128)S(1)}, f32[48,2560]{1,0:T(8,128)S(1)}, u32[]{:S(2)}, u32[]{:S(2)}) collective-permute-start(f32[48,2560]{1,0:T(8,128)S(1)} %select_add_fusion.44), channel_id=1, source_target_pairs={{4,0},{8,4},{12,8},{5,1},{9,5},{13,9},{6,2},{10,6},{14,10},{7,3},{... | collective-permute-start | bytes 1474568 | tf_op jit(solution)/shard_map/ppermute | solution.py:182
  244.2 33.7 %collective-permute-start.10 = (bf16[48,2560]{1,0:T(8,128)(2,1)S(1)}, bf16[48,2560]{1,0:T(8,128)(2,1)S(1)}, u32[]{:S(2)}, u32[]{:S(2)}) collective-permute-start(bf16[48,2560]{1,0:T(8,128)(2,1)S(1)} %get-tuple-element.273), channel_id=1, source_target_pairs={{12,8},{13,9},{14,10},{15,11},{28,24},{29,25},{30,26},{31,27}} | collective-permute-start | bytes 737288 | tf_op jit(solution)/shard_map/ppermute | solution.py:182
  244.9 33.0 %collective-permute-start.11 = (bf16[48,2560]{1,0:T(8,128)(2,1)S(1)}, bf16[48,2560]{1,0:T(8,128)(2,1)S(1)}, u32[]{:S(2)}, u32[]{:S(2)}) collective-permute-start(bf16[48,2560]{1,0:T(8,128)(2,1)S(1)} %get-tuple-element.274), channel_id=1, source_target_pairs={{0,4},{1,5},{2,6},{3,7},{16,20},{17,21},{18,22},{19,23}} | collective-permute-start | bytes 737288 | tf_op jit(solution)/shard_map/ppermute | solution.py:182
  280.2 33.0 %collective-permute-start.12 = (f32[48,2560]{1,0:T(8,128)S(1)}, f32[48,2560]{1,0:T(8,128)S(1)}, u32[]{:S(2)}, u32[]{:S(2)}) collective-permute-start(f32[48,2560]{1,0:T(8,128)S(1)} %select_add_fusion.43), channel_id=1, source_target_pairs={{0,4},{4,8},{8,12},{1,5},{5,9},{9,13},{2,6},{6,10},{10,14},{3,7},{... | collective-permute-start | bytes 1474568 | tf_op jit(solution)/shard_map/ppermute | solution.py:182
  281.6 31.6 %collective-permute-start.13 = (f32[48,2560]{1,0:T(8,128)S(1)}, f32[48,2560]{1,0:T(8,128)S(1)}, u32[]{:S(2)}, u32[]{:S(2)}) collective-permute-start(f32[48,2560]{1,0:T(8,128)S(1)} %select_add_fusion.42), channel_id=1, source_target_pairs={{4,0},{8,4},{12,8},{5,1},{9,5},{13,9},{6,2},{10,6},{14,10},{7,3},{... | collective-permute-start | bytes 1474568 | tf_op jit(solution)/shard_map/ppermute | solution.py:182
  282.9 30.3 %collective-permute-start.14 = (bf16[48,2560]{1,0:T(8,128)(2,1)S(1)}, bf16[48,2560]{1,0:T(8,128)(2,1)S(1)}, u32[]{:S(2)}, u32[]{:S(2)}) collective-permute-start(bf16[48,2560]{1,0:T(8,128)(2,1)S(1)} %get-tuple-element.288), channel_id=1, source_target_pairs={{8,4},{12,8},{9,5},{13,9},{10,6},{14,10},{11,7},{15,11},{24,20},{2... | collective-permute-start | bytes 737288 | tf_op jit(solution)/shard_map/ppermute | solution.py:182
  283.5 29.6 %collective-permute-start.15 = (bf16[48,2560]{1,0:T(8,128)(2,1)S(1)}, bf16[48,2560]{1,0:T(8,128)(2,1)S(1)}, u32[]{:S(2)}, u32[]{:S(2)}) collective-permute-start(bf16[48,2560]{1,0:T(8,128)(2,1)S(1)} %get-tuple-element.289), channel_id=1, source_target_pairs={{0,4},{4,8},{1,5},{5,9},{2,6},{6,10},{3,7},{7,11},{16,20},{20,24},... | collective-permute-start | bytes 737288 | tf_op jit(solution)/shard_map/ppermute | solution.py:182
  329.5 19.7 %collective-permute-start.16 = (f32[48,2560]{1,0:T(8,128)S(1)}, f32[48,2560]{1,0:T(8,128)S(1)}, u32[]{:S(2)}, u32[]{:S(2)}) collective-permute-start(f32[48,2560]{1,0:T(8,128)S(1)} %select_add_fusion.41), channel_id=1, source_target_pairs={{0,4},{4,8},{8,12},{1,5},{5,9},{9,13},{2,6},{6,10},{10,14},{3,7},{... | collective-permute-start | bytes 1474568 | tf_op jit(solution)/shard_map/ppermute | solution.py:182
  367.2 17.1 %collective-permute-start.20 = (f32[48,2560]{1,0:T(8,128)S(1)}, f32[48,2560]{1,0:T(8,128)S(1)}, u32[]{:S(2)}, u32[]{:S(2)}) collective-permute-start(f32[48,2560]{1,0:T(8,128)S(1)} %select_add_fusion.39), channel_id=1, source_target_pairs={{0,4},{4,8},{8,12},{1,5},{5,9},{9,13},{2,6},{6,10},{10,14},{3,7},{... | collective-permute-start | bytes 1474568 | tf_op jit(solution)/shard_map/ppermute | solution.py:182
  396.8 17.7 %collective-permute-start.24 = (f32[48,2560]{1,0:T(8,128)S(1)}, f32[48,2560]{1,0:T(8,128)S(1)}, u32[]{:S(2)}, u32[]{:S(2)}) collective-permute-start(f32[48,2560]{1,0:T(8,128)S(1)} %select_add_fusion.37), channel_id=1, source_target_pairs={{0,4},{4,8},{8,12},{1,5},{5,9},{9,13},{2,6},{6,10},{10,14},{3,7},{... | collective-permute-start | bytes 1474568 | tf_op jit(solution)/shard_map/ppermute | solution.py:182
  433.2 17.4 %collective-permute-start.28 = (f32[48,2560]{1,0:T(8,128)S(1)}, f32[48,2560]{1,0:T(8,128)S(1)}, u32[]{:S(2)}, u32[]{:S(2)}) collective-permute-start(f32[48,2560]{1,0:T(8,128)S(1)} %select_add_fusion.35), channel_id=1, source_target_pairs={{0,4},{4,8},{8,12},{1,5},{5,9},{9,13},{2,6},{6,10},{10,14},{3,7},{... | collective-permute-start | bytes 1474568 | tf_op jit(solution)/shard_map/ppermute | solution.py:182
  454.1 35.4 %collective-permute-start.32 = (f32[48,2560]{1,0:T(8,128)S(1)}, f32[48,2560]{1,0:T(8,128)}, u32[]{:S(2)}, u32[]{:S(2)}) collective-permute-start(f32[48,2560]{1,0:T(8,128)S(1)} %select_add_fusion.33), channel_id=1, source_target_pairs={{0,4},{4,8},{8,12},{1,5},{5,9},{9,13},{2,6},{6,10},{10,14},{3,7},{... | collective-permute-start | bytes 1474568 | tf_op jit(solution)/shard_map/ppermute | solution.py:182
  458.2 31.3 %collective-permute-start.33 = (f32[48,2560]{1,0:T(8,128)S(1)}, f32[48,2560]{1,0:T(8,128)}, u32[]{:S(2)}, u32[]{:S(2)}) collective-permute-start(f32[48,2560]{1,0:T(8,128)S(1)} %select_add_fusion.32), channel_id=1, source_target_pairs={{4,0},{8,4},{12,8},{5,1},{9,5},{13,9},{6,2},{10,6},{14,10},{7,3},{... | collective-permute-start | bytes 1474568 | tf_op jit(solution)/shard_map/ppermute | solution.py:182
  459.5 30.0 %collective-permute-start.34 = (bf16[48,2560]{1,0:T(8,128)(2,1)}, bf16[48,2560]{1,0:T(8,128)(2,1)}, u32[]{:S(2)}, u32[]{:S(2)}) collective-permute-start(bf16[48,2560]{1,0:T(8,128)(2,1)} %get-tuple-element.355), channel_id=1, source_target_pairs={{4,0},{8,4},{12,8},{5,1},{9,5},{13,9},{6,2},{10,6},{14,10},{7,3},{... | collective-permute-start | bytes 737288 | tf_op jit(solution)/shard_map/ppermute | solution.py:182
  460.8 28.7 %collective-permute-start.35 = (bf16[48,2560]{1,0:T(8,128)(2,1)}, bf16[48,2560]{1,0:T(8,128)(2,1)}, u32[]{:S(2)}, u32[]{:S(2)}) collective-permute-start(bf16[48,2560]{1,0:T(8,128)(2,1)} %get-tuple-element.356), channel_id=1, source_target_pairs={{0,4},{4,8},{8,12},{1,5},{5,9},{9,13},{2,6},{6,10},{10,14},{3,7},{... | collective-permute-start | bytes 737288 | tf_op jit(solution)/shard_map/ppermute | solution.py:182
  492.3 33.7 %collective-permute-start.36 = (f32[48,2560]{1,0:T(8,128)S(1)}, f32[48,2560]{1,0:T(8,128)S(1)}, u32[]{:S(2)}, u32[]{:S(2)}) collective-permute-start(f32[48,2560]{1,0:T(8,128)S(1)} %select_add_fusion.31), channel_id=1, source_target_pairs={{0,4},{4,8},{8,12},{1,5},{5,9},{9,13},{2,6},{6,10},{10,14},{3,7},{... | collective-permute-start | bytes 1474568 | tf_op jit(solution)/shard_map/ppermute | solution.py:182
  496.7 29.3 %collective-permute-start.37 = (f32[48,2560]{1,0:T(8,128)S(1)}, f32[48,2560]{1,0:T(8,128)S(1)}, u32[]{:S(2)}, u32[]{:S(2)}) collective-permute-start(f32[48,2560]{1,0:T(8,128)S(1)} %select_add_fusion.30), channel_id=1, source_target_pairs={{4,0},{8,4},{12,8},{5,1},{9,5},{13,9},{6,2},{10,6},{14,10},{7,3},{... | collective-permute-start | bytes 1474568 | tf_op jit(solution)/shard_map/ppermute | solution.py:182
  498.0 28.0 %collective-permute-start.38 = (bf16[48,2560]{1,0:T(8,128)(2,1)S(1)}, bf16[48,2560]{1,0:T(8,128)(2,1)S(1)}, u32[]{:S(2)}, u32[]{:S(2)}) collective-permute-start(bf16[48,2560]{1,0:T(8,128)(2,1)S(1)} %get-tuple-element.367), channel_id=1, source_target_pairs={{4,0},{8,4},{12,8},{5,1},{9,5},{13,9},{6,2},{10,6},{14,10},{7,3},{... | collective-permute-start | bytes 737288 | tf_op jit(solution)/shard_map/ppermute | solution.py:182
  499.3 26.7 %collective-permute-start.39 = (bf16[48,2560]{1,0:T(8,128)(2,1)S(1)}, bf16[48,2560]{1,0:T(8,128)(2,1)S(1)}, u32[]{:S(2)}, u32[]{:S(2)}) collective-permute-start(bf16[48,2560]{1,0:T(8,128)(2,1)S(1)} %get-tuple-element.368), channel_id=1, source_target_pairs={{0,4},{4,8},{8,12},{1,5},{5,9},{9,13},{2,6},{6,10},{10,14},{3,7},{... | collective-permute-start | bytes 737288 | tf_op jit(solution)/shard_map/ppermute | solution.py:182
  529.1 36.5 %collective-permute-start.40 = (f32[48,2560]{1,0:T(8,128)S(1)}, f32[48,2560]{1,0:T(8,128)S(1)}, u32[]{:S(2)}, u32[]{:S(2)}) collective-permute-start(f32[48,2560]{1,0:T(8,128)S(1)} %select_add_fusion.29), channel_id=1, source_target_pairs={{0,4},{4,8},{8,12},{1,5},{5,9},{9,13},{2,6},{6,10},{10,14},{3,7},{... | collective-permute-start | bytes 1474568 | tf_op jit(solution)/shard_map/ppermute | solution.py:182
  533.1 33.2 %collective-permute-start.41 = (f32[48,2560]{1,0:T(8,128)S(1)}, f32[48,2560]{1,0:T(8,128)S(1)}, u32[]{:S(2)}, u32[]{:S(2)}) collective-permute-start(f32[48,2560]{1,0:T(8,128)S(1)} %select_add_fusion.28), channel_id=1, source_target_pairs={{4,0},{8,4},{12,8},{5,1},{9,5},{13,9},{6,2},{10,6},{14,10},{7,3},{... | collective-permute-start | bytes 1474568 | tf_op jit(solution)/shard_map/ppermute | solution.py:182
  534.4 31.2 %collective-permute-start.42 = (bf16[48,2560]{1,0:T(8,128)(2,1)S(1)}, bf16[48,2560]{1,0:T(8,128)(2,1)S(1)}, u32[]{:S(2)}, u32[]{:S(2)}) collective-permute-start(bf16[48,2560]{1,0:T(8,128)(2,1)S(1)} %get-tuple-element.380), channel_id=1, source_target_pairs={{4,0},{8,4},{12,8},{5,1},{9,5},{13,9},{6,2},{10,6},{14,10},{7,3},{... | collective-permute-start | bytes 737288 | tf_op jit(solution)/shard_map/ppermute | solution.py:182
  535.7 29.9 %collective-permute-start.43 = (bf16[48,2560]{1,0:T(8,128)(2,1)S(1)}, bf16[48,2560]{1,0:T(8,128)(2,1)S(1)}, u32[]{:S(2)}, u32[]{:S(2)}) collective-permute-start(bf16[48,2560]{1,0:T(8,128)(2,1)S(1)} %get-tuple-element.381), channel_id=1, source_target_pairs={{0,4},{4,8},{8,12},{1,5},{5,9},{9,13},{2,6},{6,10},{10,14},{3,7},{... | collective-permute-start | bytes 737288 | tf_op jit(solution)/shard_map/ppermute | solution.py:182
  582.4 17.4 %collective-permute-start.44 = (f32[48,2560]{1,0:T(8,128)S(1)}, f32[48,2560]{1,0:T(8,128)S(1)}, u32[]{:S(2)}, u32[]{:S(2)}) collective-permute-start(f32[48,2560]{1,0:T(8,128)S(1)} %select_add_fusion.27), channel_id=1, source_target_pairs={{0,4},{4,8},{8,12},{1,5},{5,9},{9,13},{2,6},{6,10},{10,14},{3,7},{... | collective-permute-start | bytes 1474568 | tf_op jit(solution)/shard_map/ppermute | solution.py:182
  617.7 19.1 %collective-permute-start.48 = (f32[48,2560]{1,0:T(8,128)S(1)}, f32[48,2560]{1,0:T(8,128)S(1)}, u32[]{:S(2)}, u32[]{:S(2)}) collective-permute-start(f32[48,2560]{1,0:T(8,128)S(1)} %select_add_fusion.25), channel_id=1, source_target_pairs={{0,4},{4,8},{8,12},{1,5},{5,9},{9,13},{2,6},{6,10},{10,14},{3,7},{... | collective-permute-start | bytes 1474568 | tf_op jit(solution)/shard_map/ppermute | solution.py:182
  (115 other events, 2147.2 us)
Sparse Core Ops, SparseCore 0:
  17.2 24.5 all-gather.5
  157.0 32.9 all-gather.3

commit v2 on v0

v2 whole, which is shorter than its diff:
```python
import functools

import jax
import jax.numpy as jnp
from jax import lax
from jax.experimental import pallas as pl
from jax.experimental.pallas import tpu as pltpu
from jax.sharding import PartitionSpec as P

ROPE_BASE = 10000.0
NORM_EPS = 1e-6
LOG2_E = 1.4426950408889634
CHUNK = 32
LAG = 2
LAG_BACK = 2
PAIR = 2
SPLITS = 3


def rms_norm(tensor, norm_gain):
    tensor_f32 = tensor.astype(jnp.float32)
    inv_rms = lax.rsqrt(jnp.mean(tensor_f32 * tensor_f32, axis=-1, keepdims=True) + NORM_EPS)
    return (tensor_f32 * inv_rms * norm_gain).astype(jnp.bfloat16)


def rope_tables(positions, rope_dim):
    inv_freq = ROPE_BASE ** (-2.0 * jnp.arange(rope_dim // 2, dtype=jnp.float32) / rope_dim)
    angles = positions.astype(jnp.float32)[..., None] * inv_freq
    return jnp.cos(angles), jnp.sin(angles)


def rotate(tensor, cos_t, sin_t):
    tensor_f32 = tensor.astype(jnp.float32)
    half_dim = tensor_f32.shape[-1] // 2
    lower_half = tensor_f32[..., :half_dim]
    upper_half = tensor_f32[..., half_dim:]
    return jnp.concatenate([lower_half * cos_t - upper_half * sin_t,
                            lower_half * sin_t + upper_half * cos_t], axis=-1).astype(jnp.bfloat16)


def attend_kernel(soft_scale, row, order_ref, q_ref, cos_ref, sin_ref, lat_hbm, w_uk_ref, w_uv_ref, *rest):
    o_ref, lat_s, sems = rest[-3:]
    n_blocks, block_len = lat_hbm.shape[1:3]
    half_keys = n_blocks // 2 * block_len
    rank = w_uk_ref.shape[0]
    rope_dim = cos_ref.shape[1]
    nope_dim = w_uk_ref.shape[1] // PAIR
    v_dim = w_uv_ref.shape[1] // PAIR
    qk_dim = nope_dim + rope_dim

    @pl.when(pl.program_id(0) == 0)
    def _():
        copies = [pltpu.make_async_copy(lat_hbm.at[row, order_ref[j]], lat_s.at[pl.ds(j * block_len, block_len)],
                                        sems.at[j])
                  for j in range(n_blocks)]
        for copy in copies:
            copy.start()
        for copy in copies:
            copy.wait()

    low_id = order_ref[n_blocks]
    latent = lat_s[:, :rank]
    k_rope = lat_s[:, rank:rank + rope_dim]
    k_pair = jnp.dot(latent, w_uk_ref[...], preferred_element_type=jnp.float32).astype(jnp.bfloat16)
    v_pair = jnp.dot(latent, w_uv_ref[...], preferred_element_type=jnp.float32).astype(jnp.bfloat16)

    q_pair = q_ref[...].astype(jnp.float32)
    cos2 = cos_ref[...]
    sin2 = sin_ref[...]
    col_minus_row = (lax.broadcasted_iota(jnp.int32, (block_len, half_keys), 1)
                     - lax.broadcasted_iota(jnp.int32, (block_len, half_keys), 0))
    low_mask = col_minus_row <= low_id * block_len
    high_mask = col_minus_row <= (n_blocks - 1 - low_id) * block_len - half_keys
    factor = soft_scale * LOG2_E
    contract_last = (((1,), (1,)), ((), ()))

    for head in range(PAIR):
        q_head = q_pair if head == 0 else pltpu.roll(q_pair, (PAIR - head) * qk_dim, 1)
        q_rope = q_head[:, nope_dim:qk_dim]
        swapped = jnp.concatenate([q_rope[:, rope_dim // 2:], q_rope[:, :rope_dim // 2]], axis=1)
        q_rot = q_rope * cos2 + swapped * sin2
        q_cat = jnp.concatenate([q_head[:, :nope_dim], q_rot], axis=1).astype(jnp.bfloat16)
        k_cat = jnp.concatenate([k_pair[:, head * nope_dim:(head + 1) * nope_dim], k_rope], axis=1)
        v_head = v_pair[:, head * v_dim:(head + 1) * v_dim]
        early = lax.dot_general(q_cat, k_cat[:half_keys], contract_last, preferred_element_type=jnp.float32)
        late = lax.dot_general(q_cat[block_len:], k_cat[half_keys:], contract_last,
                               preferred_element_type=jnp.float32)

        low = jnp.where(low_mask, early[:block_len], -jnp.inf)
        low_exp = jnp.exp2((low - jnp.max(low, axis=1, keepdims=True)) * factor)
        low_prob = (low_exp * (1.0 / jnp.sum(low_exp, axis=1, keepdims=True))).astype(jnp.bfloat16)
        low_out = jnp.dot(low_prob, v_head[:half_keys], preferred_element_type=jnp.float32)

        near = early[block_len:]
        far = jnp.where(high_mask, late, -jnp.inf)
        top = jnp.maximum(jnp.max(near, axis=1, keepdims=True), jnp.max(far, axis=1, keepdims=True))
        near_exp = jnp.exp2((near - top) * factor)
        far_exp = jnp.exp2((far - top) * factor)
        inv_sum = 1.0 / (jnp.sum(near_exp, axis=1, keepdims=True) + jnp.sum(far_exp, axis=1, keepdims=True))
        high_out = (jnp.dot((near_exp * inv_sum).astype(jnp.bfloat16), v_head[:half_keys],
                            preferred_element_type=jnp.float32)
                    + jnp.dot((far_exp * inv_sum).astype(jnp.bfloat16), v_head[half_keys:],
                              preferred_element_type=jnp.float32))
        o_ref[:block_len, head * v_dim:(head + 1) * v_dim] = low_out.astype(jnp.bfloat16)
        o_ref[block_len:, head * v_dim:(head + 1) * v_dim] = high_out.astype(jnp.bfloat16)


def attend(q_full, cos2, sin2, lat_blocks, order, w_uk, w_uv, heads, soft_scale, row, prompt, pairs, prior):
    n_rows, n_blocks, block_len, width = lat_blocks.shape
    tokens = q_full.shape[0] // n_rows
    rank = w_uk.shape[0]
    keys = n_blocks * block_len
    qk_dim = q_full.shape[1] // heads
    nope_dim = w_uk.shape[1] // heads
    v_dim = w_uv.shape[1] // heads
    rope_dim = cos2.shape[1]
    first, count = pairs[0], len(pairs)
    flops = (2 * keys * rank * (nope_dim + v_dim) + 2 * tokens * keys * 3 // 4 * (qk_dim + v_dim)) * count * PAIR
    moved = 2 * (lat_blocks.size // n_rows + (tokens * (qk_dim + v_dim) + rank * (nope_dim + v_dim)) * count * PAIR)
    in_specs = [
        pl.BlockSpec((tokens, PAIR * qk_dim), lambda h, order: (row, h + first)),
        pl.BlockSpec((tokens, rope_dim), lambda h, order: (prompt, 0)),
        pl.BlockSpec((tokens, rope_dim), lambda h, order: (prompt, 0)),
        pl.BlockSpec(memory_space=pl.ANY),
        pl.BlockSpec((rank, PAIR * nope_dim), lambda h, order: (0, h + first)),
        pl.BlockSpec((rank, PAIR * v_dim), lambda h, order: (0, h + first)),
    ]
    operands = [q_full, cos2, sin2, lat_blocks, w_uk, w_uv]
    aliases = {}
    if prior is not None:
        in_specs.append(pl.BlockSpec(memory_space=pl.ANY))
        operands.append(prior)
        aliases = {len(operands): 0}
    return pl.pallas_call(
        functools.partial(attend_kernel, soft_scale, row),
        out_shape=jax.ShapeDtypeStruct((n_rows * tokens, heads * v_dim), jnp.bfloat16),
        grid_spec=pltpu.PrefetchScalarGridSpec(
            num_scalar_prefetch=1,
            grid=(count,),
            in_specs=in_specs,
            out_specs=pl.BlockSpec((tokens, PAIR * v_dim), lambda h, order: (row, h + first)),
            scratch_shapes=[pltpu.VMEM((keys, width), jnp.bfloat16), pltpu.SemaphoreType.DMA((n_blocks,))],
        ),
        input_output_aliases=aliases,
        compiler_params=pltpu.CompilerParams(dimension_semantics=("arbitrary",), vmem_limit_bytes=56 * 1024 * 1024),
        cost_estimate=pl.CostEstimate(flops=flops, bytes_accessed=moved,
                                      transcendentals=tokens * keys * count * PAIR * 3 // 4),
        name="attend",
    )(order, *operands)


def together(*values):
    return lax.optimization_barrier(values)


def chain_kernel(n_tp, size, attn, w_o, x_rows, out, got_up, got_dn, w_v, a_v, p_v, r_v, x_v, f_v,
                 w_sem, a_sem, r_sem, x_sem, f_sem, sum_sent, sum_got, res_sent, res_got):
    z = lax.axis_index('tp')
    last = n_tp - 1
    half = out.shape[1] // 2
    chunks = attn.shape[0] // size
    skip = out.shape[0] - attn.shape[0]
    got = (got_up, got_dn)
    place = (z, last - z)
    ahead = (z + 1, z - 1)
    behind = (z - 1, z + 1)
    first_col = (half, 0)
    tile = w_v.shape[1] // w_sem.shape[0]

    barrier = pltpu.get_barrier_semaphore()
    for there, device in ((z > 0, z - 1), (z < last, z + 1)):
        @pl.when(there)
        def _():
            pl.semaphore_signal(barrier, inc=1, device_id={'tp': device}, device_id_type=pl.DeviceIdType.MESH)
    middle = (z > 0) & (z < last)

    @pl.when(middle)
    def _():
        pl.semaphore_wait(barrier, 2)

    @pl.when(jnp.logical_not(middle))
    def _():
        pl.semaphore_wait(barrier, 1)

    def w_copy(i):
        cols = pl.ds(i * tile, tile)
        return pltpu.make_async_copy(w_o.at[:, cols], w_v.at[:, cols], w_sem.at[i])

    tiles = w_sem.shape[0]
    for i in range(tiles // 2):
        w_copy(i).start()
        w_copy(tiles // 2 + i).start()

    def rows_of(u):
        return pl.ds(pl.multiple_of(u * size, size), size)

    def out_rows(u):
        return pl.ds(pl.multiple_of(skip + u * size, size), size)

    def a_copy(d, u):
        slot = lax.rem(u, 2)
        return pltpu.make_async_copy(attn.at[rows_of(u)], a_v.at[d, slot], a_sem.at[d, slot])

    def r_copy(d, u):
        return pltpu.make_async_copy(got[d].at[rows_of(u)], r_v.at[d], r_sem.at[d])

    def x_copy(d, u):
        return pltpu.make_async_copy(x_rows.at[out_rows(u), pl.ds(first_col[d], half)], x_v.at[d], x_sem.at[d])

    def f_copy(d, u):
        slot = lax.rem(u, 2)
        return pltpu.make_async_copy(f_v.at[d, slot], out.at[out_rows(u), pl.ds(first_col[d], half)],
                                     f_sem.at[d, slot])

    def sum_send(d, u):
        return pltpu.make_async_remote_copy(
            src_ref=p_v.at[d, lax.rem(u, 2)], dst_ref=got[d].at[rows_of(u)],
            send_sem=sum_sent.at[d, u], recv_sem=sum_got.at[d, u],
            device_id={'tp': ahead[d]}, device_id_type=pl.DeviceIdType.MESH)

    def res_first(d, u):
        return pltpu.make_async_remote_copy(
            src_ref=f_v.at[d, lax.rem(u, 2)], dst_ref=out.at[out_rows(u), pl.ds(first_col[d], half)],
            send_sem=res_sent.at[d, u], recv_sem=res_got.at[d, u],
            device_id={'tp': behind[d]}, device_id_type=pl.DeviceIdType.MESH)

    def res_pass(d, u):
        here = out.at[out_rows(u), pl.ds(first_col[d], half)]
        return pltpu.make_async_remote_copy(
            src_ref=here, dst_ref=here, send_sem=res_sent.at[d, u], recv_sem=res_got.at[d, u],
            device_id={'tp': behind[d]}, device_id_type=pl.DeviceIdType.MESH)

    def inside(u):
        return (u >= 0) & (u < chunks)

    def step(index, carry):
        t = index - 2
        chunk = [t - LAG * place[d] for d in range(2)]
        for d in range(2):
            u = chunk[d]

            @pl.when(inside(u) & (place[d] > 0))
            def _():
                sum_send(d, u).wait_recv()
                r_copy(d, u).start()

            @pl.when(inside(u) & (place[d] == last))
            def _():
                x_copy(d, u).start()

        for d in range(2):
            u = chunk[d]
            slot = lax.rem(u + 2, 2)

            @pl.when(inside(u) & (place[d] > 0))
            def _():
                r_copy(d, u).wait()

            @pl.when(inside(u) & (place[d] > 0) & (place[d] < last))
            def _():
                p_v[d, slot] = p_v[d, slot] + r_v[d]

            @pl.when(inside(u) & (place[d] < last))
            def _():
                sum_send(d, u).start()

            @pl.when(inside(u) & (place[d] == last))
            def _():
                x_copy(d, u).wait()
                f_v[d, slot] = (x_v[d].astype(jnp.float32) + (p_v[d, slot] + r_v[d])).astype(jnp.bfloat16)
                f_copy(d, u).start()
                res_first(d, u).start()

        for d in range(2):
            v = t - LAG * last - LAG_BACK * (last - place[d])

            @pl.when(inside(v) & (place[d] > 0) & (place[d] < last))
            def _():
                res_pass(d, v).wait_recv()
                res_pass(d, v).start()

        @pl.when(t == -1)
        def _():
            for i in range(tiles):
                w_copy(i).wait()

        for d in range(2):
            u = chunk[d]

            @pl.when(inside(u + 2))
            def _():
                a_copy(d, u + 2).start()

            @pl.when(inside(u + 1))
            def _():
                slot = lax.rem(u + 1, 2)

                @pl.when(inside(u - 1) & (place[d] < last))
                def _():
                    sum_send(d, u - 1).wait_send()

                @pl.when(inside(u - 1) & (place[d] == last))
                def _():
                    f_copy(d, u - 1).wait()
                    res_first(d, u - 1).wait_send()

                a_copy(d, u + 1).wait()

                def column_tile(j, carry):
                    cols = pl.ds(pl.multiple_of(j * tile, tile), tile)
                    w_cols = pl.ds(pl.multiple_of(first_col[d] + j * tile, tile), tile)
                    p_v[d, slot, :, cols] = jnp.dot(a_v[d, slot], w_v[:, w_cols], preferred_element_type=jnp.float32)
                    return carry

                lax.fori_loop(0, tiles // 2, column_tile, 0)
        return carry

    lax.fori_loop(0, chunks + 2 + LAG * last + LAG_BACK * (last - 1), step, 0)

    for d in range(2):
        for u in (chunks - 2, chunks - 1):
            @pl.when(place[d] < last)
            def _():
                sum_send(d, u).wait_send()

            @pl.when(place[d] == last)
            def _():
                f_copy(d, u).wait()
                res_first(d, u).wait_send()

        def drain(u, carry):
            @pl.when((place[d] > 0) & (place[d] < last))
            def _():
                res_pass(d, u).wait_send()

            @pl.when(place[d] == 0)
            def _():
                res_pass(d, u).wait_recv()
            return carry

        lax.fori_loop(0, chunks, drain, 0)


def chain_sum(attn, w_o, x_rows, n_tp, size):
    rows, inner = attn.shape
    width = w_o.shape[1]
    half = width // 2
    chunks = rows // size
    tiles = 2 * max(1, half // 512)
    sems = pltpu.SemaphoreType.DMA
    out, _, _ = pl.pallas_call(
        functools.partial(chain_kernel, n_tp, size),
        out_shape=(jax.ShapeDtypeStruct(x_rows.shape, jnp.bfloat16),
                   jax.ShapeDtypeStruct((rows, half), jnp.float32),
                   jax.ShapeDtypeStruct((rows, half), jnp.float32)),
        in_specs=[pl.BlockSpec(memory_space=pl.ANY)] * 3,
        out_specs=(pl.BlockSpec(memory_space=pl.ANY),) * 3,
        scratch_shapes=[
            pltpu.VMEM((inner, width), jnp.bfloat16),
            pltpu.VMEM((2, 2, size, inner), jnp.bfloat16),
            pltpu.VMEM((2, 2, size, half), jnp.float32),
            pltpu.VMEM((2, size, half), jnp.float32),
            pltpu.VMEM((2, size, half), jnp.bfloat16),
            pltpu.VMEM((2, 2, size, half), jnp.bfloat16),
            sems((tiles,)), sems((2, 2)), sems((2,)), sems((2,)), sems((2, 2)),
            sems((2, chunks)), sems((2, chunks)), sems((2, chunks)), sems((2, chunks)),
        ],
        compiler_params=pltpu.CompilerParams(collective_id=0, has_side_effects=True,
                                             vmem_limit_bytes=60 * 1024 * 1024),
        cost_estimate=pl.CostEstimate(flops=2 * rows * inner * width, transcendentals=0,
                                      bytes_accessed=2 * inner * width + 12 * rows * width),
        name="chain_sum",
    )(attn, w_o, x_rows)
    return out


def solution(mesh):
    n_tp = mesh.shape['tp']
    n_cp = mesh.shape['cp']

    def local_step(x_blk, pos_blk, w_dq, g_q, w_uq, w_dkv, g_kv, w_uk, w_uv, w_o):
        num_seq, seq_dev, width = x_blk.shape
        kv_rank = g_kv.shape[0]
        rope_dim = w_dkv.shape[1] - kv_rank
        heads_dev = (w_uq.shape[1] - w_uk.shape[1]) // rope_dim
        nope_dim = w_uk.shape[1] // heads_dev
        soft_scale = (nope_dim + rope_dim) ** -0.5
        n_blocks = 2 * n_cp
        block_len = seq_dev // 2
        n_pairs = heads_dev // PAIR
        cuts = [n_pairs * i // SPLITS for i in range(SPLITS + 1)]
        pos_f32 = pos_blk.astype(jnp.float32)
        x_flat = x_blk.reshape(num_seq * seq_dev, width)

        cos_t, sin_t = rope_tables(pos_f32.reshape(-1), rope_dim)
        tables = (jnp.concatenate([cos_t, cos_t], axis=1), jnp.concatenate([-sin_t, sin_t], axis=1))
        kv_joint = jnp.dot(x_flat, w_dkv, preferred_element_type=jnp.float32).astype(jnp.bfloat16)
        latent = rms_norm(kv_joint[:, :kv_rank], g_kv)
        k_rope = rotate(kv_joint[:, kv_rank:], cos_t, sin_t)
        block_ids = jnp.floor(pos_f32.reshape(-1) / block_len)[:, None].astype(jnp.bfloat16)
        both = jnp.concatenate([latent, k_rope, jnp.broadcast_to(block_ids, k_rope.shape)], axis=1)
        both = both.reshape(num_seq, seq_dev, -1)

        def gather(lo, hi):
            everyone = lax.all_gather(both[lo:hi], 'cp', axis=1, tiled=True).reshape(hi - lo, n_blocks, block_len, -1)
            ids_all = everyone[:, :, 0, kv_rank + rope_dim].astype(jnp.int32)
            blocks = jnp.arange(n_blocks, dtype=jnp.int32)
            where = jnp.sum(jnp.where(ids_all[:, None, :] == blocks[:, None], blocks, 0), axis=2)
            order = jnp.concatenate([where, pos_blk[lo:hi, :1] // block_len], axis=1).astype(jnp.int32)
            return everyone, order

        def q_of(rows):
            q_latent = jnp.dot(rows, w_dq, preferred_element_type=jnp.float32).astype(jnp.bfloat16)
            return jnp.dot(rms_norm(q_latent, g_q), w_uq, preferred_element_type=jnp.float32).astype(jnp.bfloat16)

        x_first, x_rest = x_flat[:seq_dev], x_flat[seq_dev:]
        everyone, order = gather(0, 1)
        everyone_r, order_r = gather(1, num_seq)
        attn = attend(q_of(x_first), *tables, everyone, order[0], w_uk, w_uv, heads_dev, soft_scale, 0, 0,
                      range(n_pairs), None)
        share = jnp.dot(attn, w_o, preferred_element_type=jnp.float32)
        x_rest, share = together(x_rest, share)
        mine = lax.psum_scatter(share, 'tp', scatter_dimension=0, tiled=True)
        q_rest = q_of(x_rest)
        attn = None
        for n in range(num_seq - 1):
            for i in range(SPLITS):
                attn = attend(q_rest, *tables, everyone_r, order_r[n], w_uk, w_uv, heads_dev, soft_scale, n, n + 1,
                              range(cuts[i], cuts[i + 1]), attn)
                if n == num_seq - 2 and i == 0:
                    attn, mine = together(attn, mine)
                    own = mine.shape[0]
                    x_own = lax.dynamic_slice(x_first, (lax.axis_index('tp') * own, 0), (own, width))
                    first_own = (x_own.astype(jnp.float32) + mine).astype(jnp.bfloat16)
                    out_first = lax.all_gather(first_own, 'tp', axis=0, tiled=True)
        out = chain_sum(attn, w_o, x_flat, n_tp, CHUNK)
        out = lax.dynamic_update_slice(out, out_first, (0, 0)).reshape(x_blk.shape)
        return out, latent.reshape(num_seq, seq_dev, -1), k_rope.reshape(num_seq, seq_dev, -1)

    seq_spec = P('dp', 'cp', None)
    in_specs = (seq_spec, P('dp', 'cp'), P(None, None), P(None), P(None, 'tp'), P(None, None), P(None),
                P(None, 'tp'), P(None, 'tp'), P('tp', None))
    return jax.shard_map(local_step, mesh=mesh, in_specs=in_specs,
                         out_specs=(seq_spec, seq_spec, seq_spec), check_vma=False)
```

time: 1450 us -> 680 us (0.47)
  waiting for transfers between devices: 866 us -> 16 us
  Pallas kernels: 0 us -> 500 us
  matrix products: 475 us -> 98.9 us
  blocking collectives: 18.2 us -> 0 us
  local copies, waits for them, and re-layouts: 44.4 us -> 28.4 us
    psum x1 -> x0, waiting for transfers between devices: 776 us -> none  [local_step(): head_sum = lax.psum(part_out, 'tp')]
    pallas_call x0 -> x8, Pallas kernels: none -> 500 us  [the longest x1 329 us: chain_sum(): pl.pallas_call(functools.partial(chain_kernel, n_tp, size), out_shape=(ja...]
    dot_general x8 -> x6, matrix products: 297 us -> 98.9 us  [the longest x2 29.4 us: q_of(): jnp.dot(rows, w_dq, preferred_element_type=jnp.float32).astype(jnp.bfloat16)]
    sub x1 -> x0, matrix products: 177 us -> none  [attend(): probs_bf = jax.nn.softmax(scores, axis=-1).astype(jnp.bfloat16)]
    all_gather x2 -> x3, waiting for transfers between devices: 89.2 us -> 0.02 us  [the longest x1 0.02 us: local_step(): out_first = lax.all_gather(first_own, 'tp', axis=0, tiled=True)]
    reshape x2 -> x0, local copies, waits for them, and re-layouts: 22.6 us -> none  [the longest x1 12.7 us: local_step(): values = values.reshape(num_seq, seq_dev, heads_dev, v_dim)]
    convert_element_type x1 -> x0, local copies, waits for them, and re-layouts: 18.6 us -> none  [local_step(): q_full = jnp.einsum('nsr,rk->nsk', rms_norm(q_latent, g_q), w_uq, preferr...]
    all_gather x2 -> x0, blocking collectives: 18.2 us -> none  [the longest x1 11.7 us: local_step(): k_rope_all = lax.all_gather(k_rope, 'cp', axis=1, tiled=True)]
  transfers between devices with their start and end apart: 3 -> 4, of which waited for: 3 -> 1; matrix products, arithmetic and copies ran while one was open for 25% -> 15% of each run, Pallas kernels for 0% -> 74%
where the time goes in v2:
time: 680 us; the launch traced here: 674 us
  Pallas kernels  500 us (74%)
  matrix products  98.9 us (15%)
  local copies, waits for them, and re-layouts  28.4 us (4%)
  between operations  16.3 us (2%)
  waiting for transfers between devices  16 us (2%)
  other arithmetic  13.8 us (2%)
    pallas_call x1, Pallas kernels, chain_sum(): pl.pallas_call(functools.partial(chain_kernel, n_tp, size), out_shape=(ja...  329 us
    pallas_call x7, Pallas kernels, attend(): pl.pallas_call(functools.partial(attend_kernel, soft_scale, row), out_sha...  172 us
    dot_general x2, matrix products, q_of(): jnp.dot(rows, w_dq, preferred_element_type=jnp.float32).astype(jnp.bfloat16)  29.4 us
    dot_general x2, matrix products, q_of(): jnp.dot(rms_norm(q_latent, g_q), w_uq, preferred_element_type=jnp.float32)  29.1 us
    dot_general x1, matrix products, local_step(): share = jnp.dot(attn, w_o, preferred_element_type=jnp.float32)  26.4 us
    reduce_scatter x1, waiting for transfers between devices, local_step(): mine = lax.psum_scatter(share, 'tp', scatter_dimension=0, tiled=True)  15.9 us
    dot_general x1, matrix products, local_step(): jnp.dot(x_flat, w_dkv, preferred_element_type=jnp.float32)  14 us
  transfers between devices with their start and end apart: 4, of which 1 were waited for; matrix products, arithmetic and copies ran while one was open for 15% of the time, Pallas kernels for 74%

profile of v2, /device:TPU:0, one launch (start us, length us, event | category | flops | bytes accessed | tf_op | source)
XLA Modules:
  0.0 674.2 jit_solution(4197093978218529458)
XLA Ops:
  7.2 14.0 %convolution_convert_fusion.3 = bf16[1152,576]{1,0:T(8,128)(2,1)S(1)} fusion(bf16[1152,5120]{1,0:T(8,128)(2,1)} %bitcast.42, bf16[5120,576]{0,1:T(8,128)(2,1)} %param.15), kind=kOutput, calls=%fused_computation.10 | convolution fusion | flops 6795436032 | bytes 19021824 | tf_op jit(solution)/shard_map/dot_general | solution.py:397
  21.6 3.6 fusion.21
  25.2 0.3 fusion.10
  25.8 0.9 pad_maximum_fusion.3
  26.8 0.3 pad_maximum_fusion
  27.2 1.1 slice.80
  28.3 0.5 slice.72
  30.8 7.2 %slice.67 = bf16[2,384,5120]{2,1,0:T(8,128)(2,1)} slice(bf16[3,384,5120]{2,1,0:T(8,128)(2,1)} %param.10), slice={[1:3], [0:384], [0:5120]} | slice | bytes 15728640 | tf_op jit(solution)/shard_map/slice | solution.py:416
  38.0 11.7 %fusion.11 = (f32[384]{0:T(512)S(1)}, bf16[384,1536]{1,0:T(8,128)(2,1)S(1)}) fusion(bf16[5120,1536]{1,0:T(8,128)(2,1)} %param.12, bf16[3,384,5120]{2,1,0:T(8,128)(2,1)} %param.10), kind=kOutput, calls=%fused_computation.19 | convolution fusion | flops 6042156544 | bytes 20841984 | tf_op jit(solution)/shard_map/dot_general | solution.py:413
  49.8 1.4 pad_maximum_fusion.1
  51.2 9.4 %convolution_convert_fusion.1.q_ref = bf16[384,6144]{1,0:T(8,128)(2,1)} fusion(bf16[1536,6144]{1,0:T(8,128)(2,1)S(1)} %bitcast.53, bf16[384,1536]{1,0:T(8,128)(2,1)S(1)} %get-tuple-element.23, f32[1536]{0:T(1024)S(1)} %copy-done.10, f32[384]{0:T(512)S(1)} %add_rsqrt_fusion.2), kind=kOutput, calls=%fused_computation.1 | convolution fusion | flops 7252475904 | bytes 24780288 | tf_op jit(solution)/shard_map/dot_general | solution.py:414
  60.6 1.0 fusion.29
  61.7 0.6 add_bitcast_fusion.order_ref
  62.3 51.4 %attend.7 = bf16[384,4096]{1,0:T(8,128)(2,1)} custom-call(s32[9]{0:T(128)} %add_bitcast_fusion.order_ref, bf16[384,6144]{1,0:T(8,128)(2,1)} %convolution_convert_fusion.1.q_ref, f32[1152,64]{1,0:T(8,128)} %get-tuple-element.26.cos_ref, f32[1152,64]{1,0:T(8,128)} %get-tuple-element.27.sin_ref, bf16[1,8,192,640]{3,2,1,0:T(8,128)(2,1)} %bitcast.51, ...), custom_call_target="tpu_custom_call" | custom-call | flops 21944598528 | bytes 18219008 | tf_op jit(solution)/shard_map/attend/pallas_call | solution.py:134
  113.8 26.4 %fusion.31 = f32[384,5120]{1,0:T(8,128)} fusion(bf16[384,4096]{1,0:T(8,128)(2,1)} %attend.7, bf16[4096,5120]{1,0:T(8,128)(2,1)} %w_o.1), kind=kOutput, calls=%fused_computation.63 | convolution fusion | flops 16106127360 | bytes 52953088 | tf_op jit(solution)/shard_map/dot_general | solution.py:421
  140.4 4.3 slice.73
  144.7 17.8 %fusion = (f32[768]{0:T(1024)S(1)}, bf16[768,1536]{1,0:T(8,128)(2,1)S(1)}) fusion(bf16[768,5120]{1,0:T(8,128)(2,1)} %bitcast.46, bf16[5120,1536]{1,0:T(8,128)(2,1)} %param.12), kind=kOutput, calls=%fused_computation.4 | convolution fusion | flops 12084313088 | bytes 25955328 | tf_op jit(solution)/shard_map/dot_general | solution.py:413
  162.5 19.7 %convolution_convert_fusion.q_ref = bf16[768,6144]{1,0:T(8,128)(2,1)} fusion(bf16[1536,6144]{1,0:T(8,128)(2,1)} %param.14, bf16[768,1536]{1,0:T(8,128)(2,1)S(1)} %get-tuple-element.25, f32[1536]{0:T(1024)S(1)} %copy-done.10, f32[768]{0:T(1024)S(1)} %add_rsqrt_fusion.1), kind=kOutput, calls=%fused_computation | convolution fusion | flops 14504951808 | bytes 30680064 | tf_op jit(solution)/shard_map/dot_general | solution.py:414
  182.2 1.2 fusion.28
  183.7 0.5 slice_bitcast_fusion
  184.2 19.0 %attend.8.rest_0_ = bf16[768,4096]{1,0:T(8,128)(2,1)} custom-call(s32[9]{0:T(128)} %get-tuple-element.20.order_ref, bf16[768,6144]{1,0:T(8,128)(2,1)} %convolution_convert_fusion.q_ref, f32[1152,64]{1,0:T(8,128)} %get-tuple-element.26.cos_ref, f32[1152,64]{1,0:T(8,128)} %get-tuple-element.27.sin_ref, bf16[2,8,192,640]{3,2,1,0:T(8,128)(2,1)} %bitcast.36, ...), custom_call_target="tpu_custom_call" | custom-call | flops 6857687040 | bytes 7045120 | tf_op jit(solution)/shard_map/attend/pallas_call | solution.py:134
  203.2 19.0 %attend.9.rest_0_ = bf16[768,4096]{1,0:T(8,128)(2,1)} custom-call(s32[9]{0:T(128)} %get-tuple-element.20.order_ref, bf16[768,6144]{1,0:T(8,128)(2,1)} %convolution_convert_fusion.q_ref, f32[1152,64]{1,0:T(8,128)} %get-tuple-element.26.cos_ref, f32[1152,64]{1,0:T(8,128)} %get-tuple-element.27.sin_ref, ...), custom_call_target="tpu_custom_call", output_to_operand_aliasing={{}: (7, {})} | custom-call | flops 6857687040 | bytes 7045120 | tf_op jit(solution)/shard_map/attend/pallas_call | solution.py:134
  222.2 22.2 %attend.10.rest_0_ = bf16[768,4096]{1,0:T(8,128)(2,1)} custom-call(s32[9]{0:T(128)} %get-tuple-element.20.order_ref, bf16[768,6144]{1,0:T(8,128)(2,1)} %convolution_convert_fusion.q_ref, f32[1152,64]{1,0:T(8,128)} %get-tuple-element.26.cos_ref, f32[1152,64]{1,0:T(8,128)} %get-tuple-element.27.sin_ref, ...), custom_call_target="tpu_custom_call", output_to_operand_aliasing={{}: (7, {})} | custom-call | flops 8229224448 | bytes 8060928 | tf_op jit(solution)/shard_map/attend/pallas_call | solution.py:134
  244.4 19.0 %attend.11.rest_0_ = bf16[768,4096]{1,0:T(8,128)(2,1)} custom-call(s32[9]{0:T(128)} %get-tuple-element.21.order_ref, bf16[768,6144]{1,0:T(8,128)(2,1)} %convolution_convert_fusion.q_ref, f32[1152,64]{1,0:T(8,128)} %get-tuple-element.26.cos_ref, f32[1152,64]{1,0:T(8,128)} %get-tuple-element.27.sin_ref, ...), custom_call_target="tpu_custom_call", output_to_operand_aliasing={{}: (7, {})} | custom-call | flops 6857687040 | bytes 7045120 | tf_op jit(solution)/shard_map/attend/pallas_call | solution.py:134
  263.4 15.9 %reduce-scatter.2.cloned.1.call-done = f32[96,5120]{1,0:T(8,128)} async-done(((f32[384,5120]{1,0:T(8,128)}), f32[96,5120]{1,0:T(8,128)}) %reduce-scatter.2.cloned.1.call-update) | async-done | bytes 1966096 | tf_op jit(solution)/shard_map/reduce_scatter | solution.py:423
  279.4 2.9 fusion.17
  282.7 0.7 pad_maximum_fusion.4
  283.4 19.0 %attend.12.rest_0_ = bf16[768,4096]{1,0:T(8,128)(2,1)} custom-call(s32[9]{0:T(128)} %get-tuple-element.21.order_ref, bf16[768,6144]{1,0:T(8,128)(2,1)} %convolution_convert_fusion.q_ref, f32[1152,64]{1,0:T(8,128)} %get-tuple-element.26.cos_ref, f32[1152,64]{1,0:T(8,128)} %get-tuple-element.27.sin_ref, ...), custom_call_target="tpu_custom_call", output_to_operand_aliasing={{}: (7, {})} | custom-call | flops 6857687040 | bytes 7045120 | tf_op jit(solution)/shard_map/attend/pallas_call | solution.py:134
  302.4 22.0 %attend.13.attn = bf16[768,4096]{1,0:T(8,128)(2,1)} custom-call(s32[9]{0:T(128)} %get-tuple-element.21.order_ref, bf16[768,6144]{1,0:T(8,128)(2,1)} %convolution_convert_fusion.q_ref, f32[1152,64]{1,0:T(8,128)} %get-tuple-element.26.cos_ref, f32[1152,64]{1,0:T(8,128)} %get-tuple-element.27.sin_ref, ...), custom_call_target="tpu_custom_call", output_to_operand_aliasing={{}: (7, {})} | custom-call | flops 8229224448 | bytes 8060928 | tf_op jit(solution)/shard_map/attend/pallas_call | solution.py:134
  324.4 328.8 %chain_sum.1 = (bf16[1152,5120]{1,0:T(8,128)(2,1)}, f32[768,2560]{1,0:T(8,128)}, f32[768,2560]{1,0:T(8,128)}) custom-call(bf16[768,4096]{1,0:T(8,128)(2,1)} %attend.13.attn, bf16[4096,5120]{1,0:T(8,128)(2,1)} %w_o.1, bf16[1152,5120]{1,0:T(8,128)(2,1)} %bitcast.43), custom_call_target="tpu_custom_call" | custom-call | flops 32212254720 | bytes 89128960 | tf_op jit(solution)/shard_map/chain_sum/pallas_call | solution.py:351
  653.2 4.2 constant_dynamic-update-slice_fusion
  657.4 10.0 %copy.35 = bf16[3,384,5120]{2,1,0:T(8,128)(2,1)} copy(bf16[3,384,5120]{2,1,0:T(8,128)(2,1)} %bitcast.44) | data formatting | bytes 23592960
  (60 shorter events, 1.8 us)
Async XLA Ops:
  7.2 53.4 %all-gather.9.cloned.1.call-start = ((), (), s32[]{:S(2)}) async-start(), calls=%async_computation.4 | async-start | bytes 2457600 | tf_op jit(solution)/shard_map/all_gather | solution.py:405
  7.2 14.4 %copy-start.8 = (s32[3,384]{1,0:T(4,128)S(1)}, s32[3,384]{1,0:T(4,128)}, u32[]{:S(2)}) copy-start(s32[3,384]{1,0:T(4,128)} %param.11) | copy-start | bytes 13828
  21.2 4.0 copy-start.9
  25.2 1.9 copy-start.1
  25.2 1.9 copy-start.3
  25.6 2.7 copy-start
  26.8 155.5 %all-gather.5.cloned.1.call-start = ((), (), s32[]{:S(2)}) async-start(), calls=%async_computation.1 | async-start | bytes 4915200 | tf_op jit(solution)/shard_map/all_gather | solution.py:405
  28.3 251.1 %reduce-scatter.2.cloned.1.call-start = ((), (), s32[]{:S(2)}) async-start(), calls=%async_computation.2 | async-start | bytes 9830400 | tf_op jit(solution)/shard_map/reduce_scatter | solution.py:423
  30.8 20.4 %slice-start = ((s8[18874368]{0:T(1024)(128)(4,1)}), s8[2097152]{0:T(1024)(128)(4,1)S(1)}, s32[]{:S(2)}) async-start(s8[18874368]{0:T(1024)(128)(4,1)} %bitcast.52), calls=%async_computation.5 | async-start | bytes 4194304
  30.8 20.4 %slice-start.1 = ((s8[18874368]{0:T(1024)(128)(4,1)}), s8[4194304]{0:T(1024)(128)(4,1)S(1)}, s32[]{:S(2)}) async-start(s8[18874368]{0:T(1024)(128)(4,1)} %bitcast.52), calls=%async_computation.6 | async-start | bytes 8388608
  38.0 11.8 %copy-start.5 = (f32[1152,32]{1,0:T(8,128)S(1)}, f32[1152,32]{1,0:T(8,128)}, u32[]{:S(2)}) copy-start(f32[1152,32]{1,0:T(8,128)} %get-tuple-element.15) | copy-start | bytes 442372
  38.0 11.8 %copy-start.6 = (f32[1152,32]{1,0:T(8,128)S(1)}, f32[1152,32]{1,0:T(8,128)}, u32[]{:S(2)}) copy-start(f32[1152,32]{1,0:T(8,128)} %get-tuple-element.16) | copy-start | bytes 442372
  38.0 11.8 %copy-start.7 = (f32[1152,32]{1,0:T(8,128)S(1)}, f32[1152,32]{1,0:T(8,128)}, u32[]{:S(2)}) copy-start(f32[1152,32]{1,0:T(8,128)} %get-tuple-element.19) | copy-start | bytes 442372
  38.0 13.2 %slice-start.2 = ((s8[18874368]{0:T(1024)(128)(4,1)}), s8[4194304]{0:T(1024)(128)(4,1)S(1)}, s32[]{:S(2)}) async-start(s8[18874368]{0:T(1024)(128)(4,1)} %bitcast.52), calls=%async_computation.7 | async-start | bytes 8388608
  38.0 13.2 %slice-start.3 = ((s8[18874368]{0:T(1024)(128)(4,1)}), s8[4194304]{0:T(1024)(128)(4,1)S(1)}, s32[]{:S(2)}) async-start(s8[18874368]{0:T(1024)(128)(4,1)} %bitcast.52), calls=%async_computation.8 | async-start | bytes 8388608
  38.0 13.2 %slice-start.4 = ((s8[18874368]{0:T(1024)(128)(4,1)}), s8[4194304]{0:T(1024)(128)(4,1)S(1)}, s32[]{:S(2)}) async-start(s8[18874368]{0:T(1024)(128)(4,1)} %bitcast.52), calls=%async_computation.9 | async-start | bytes 8388608
  38.0 13.2 %copy-start.10 = (f32[1536]{0:T(1024)S(1)}, f32[1536]{0:T(1024)}, u32[]{:S(2)}) copy-start(f32[1536]{0:T(1024)} %param.13) | copy-start | bytes 18436
  140.2 513.0 %all-gather.7.cloned.1.call-start = ((), (), s32[]{:S(2)}) async-start(), calls=%async_computation.3 | async-start | bytes 4915200 | tf_op jit(solution)/shard_map/all_gather | solution.py:435
  263.4 18.9 %copy-start.4 = (bf16[1152,32]{1,0:T(8,128)(2,1)S(1)}, bf16[1152,32]{1,0:T(8,128)(2,1)}, u32[]{:S(2)}) copy-start(bf16[1152,32]{1,0:T(8,128)(2,1)} %copy-done.3) | copy-start | bytes 221188
  263.4 19.1 %copy-start.2 = (bf16[1152,32]{1,0:T(8,128)(2,1)S(1)}, bf16[1152,32]{1,0:T(8,128)(2,1)}, u32[]{:S(2)}) copy-start(bf16[1152,32]{1,0:T(8,128)(2,1)} %copy-done.1) | copy-start | bytes 221188
Sparse Core Ops, SparseCore 0:
  26.9 24.3 all-gather.8
  52.8 32.7 all-gather.4
  140.3 139.0 reduce-scatter.1
  282.5 84.8 all-gather.6

commit v3 on v2

--- a/solution.py
+++ b/solution.py
@@ -14,7 +14,6 @@
 LAG = 2
 LAG_BACK = 2
 PAIR = 2
-SPLITS = 3
 
 
 def rms_norm(tensor, norm_gain):
@@ -62,7 +61,6 @@
     latent = lat_s[:, :rank]
     k_rope = lat_s[:, rank:rank + rope_dim]
     k_pair = jnp.dot(latent, w_uk_ref[...], preferred_element_type=jnp.float32).astype(jnp.bfloat16)
-    v_pair = jnp.dot(latent, w_uv_ref[...], preferred_element_type=jnp.float32).astype(jnp.bfloat16)
 
     q_pair = q_ref[...].astype(jnp.float32)
     cos2 = cos_ref[...]
@@ -74,35 +72,54 @@
     factor = soft_scale * LOG2_E
     contract_last = (((1,), (1,)), ((), ()))
 
-    for head in range(PAIR):
+    def scores(head):
         q_head = q_pair if head == 0 else pltpu.roll(q_pair, (PAIR - head) * qk_dim, 1)
         q_rope = q_head[:, nope_dim:qk_dim]
         swapped = jnp.concatenate([q_rope[:, rope_dim // 2:], q_rope[:, :rope_dim // 2]], axis=1)
         q_rot = q_rope * cos2 + swapped * sin2
         q_cat = jnp.concatenate([q_head[:, :nope_dim], q_rot], axis=1).astype(jnp.bfloat16)
         k_cat = jnp.concatenate([k_pair[:, head * nope_dim:(head + 1) * nope_dim], k_rope], axis=1)
-        v_head = v_pair[:, head * v_dim:(head + 1) * v_dim]
         early = lax.dot_general(q_cat, k_cat[:half_keys], contract_last, preferred_element_type=jnp.float32)
         late = lax.dot_general(q_cat[block_len:], k_cat[half_keys:], contract_last,
                                preferred_element_type=jnp.float32)
-
+        return early, late
+
+    def low_probs(early):
         low = jnp.where(low_mask, early[:block_len], -jnp.inf)
         low_exp = jnp.exp2((low - jnp.max(low, axis=1, keepdims=True)) * factor)
-        low_prob = (low_exp * (1.0 / jnp.sum(low_exp, axis=1, keepdims=True))).astype(jnp.bfloat16)
-        low_out = jnp.dot(low_prob, v_head[:half_keys], preferred_element_type=jnp.float32)
-
+        return (low_exp * (1.0 / jnp.sum(low_exp, axis=1, keepdims=True))).astype(jnp.bfloat16)
+
+    def high_probs(early, late):
         near = early[block_len:]
         far = jnp.where(high_mask, late, -jnp.inf)
         top = jnp.maximum(jnp.max(near, axis=1, keepdims=True), jnp.max(far, axis=1, keepdims=True))
         near_exp = jnp.exp2((near - top) * factor)
         far_exp = jnp.exp2((far - top) * factor)
         inv_sum = 1.0 / (jnp.sum(near_exp, axis=1, keepdims=True) + jnp.sum(far_exp, axis=1, keepdims=True))
-        high_out = (jnp.dot((near_exp * inv_sum).astype(jnp.bfloat16), v_head[:half_keys],
-                            preferred_element_type=jnp.float32)
-                    + jnp.dot((far_exp * inv_sum).astype(jnp.bfloat16), v_head[half_keys:],
-                              preferred_element_type=jnp.float32))
-        o_ref[:block_len, head * v_dim:(head + 1) * v_dim] = low_out.astype(jnp.bfloat16)
-        o_ref[block_len:, head * v_dim:(head + 1) * v_dim] = high_out.astype(jnp.bfloat16)
+        return (near_exp * inv_sum).astype(jnp.bfloat16), (far_exp * inv_sum).astype(jnp.bfloat16)
+
+    def low_value(head, probs):
+        cols = slice(head * v_dim, (head + 1) * v_dim)
+        o_ref[:block_len, cols] = jnp.dot(probs, v_pair[:half_keys, cols],
+                                          preferred_element_type=jnp.float32).astype(jnp.bfloat16)
+
+    def high_value(head, near, far):
+        cols = slice(head * v_dim, (head + 1) * v_dim)
+        o_ref[block_len:, cols] = (jnp.dot(near, v_pair[:half_keys, cols], preferred_element_type=jnp.float32)
+                                   + jnp.dot(far, v_pair[half_keys:, cols],
+                                             preferred_element_type=jnp.float32)).astype(jnp.bfloat16)
+
+    first = scores(0)
+    v_pair = jnp.dot(latent, w_uv_ref[...], preferred_element_type=jnp.float32).astype(jnp.bfloat16)
+    low = low_probs(first[0])
+    second = scores(1)
+    high = high_probs(*first)
+    low_value(0, low)
+    low = low_probs(second[0])
+    high_value(0, *high)
+    high = high_probs(*second)
+    low_value(1, low)
+    high_value(1, *high)
 
 
 def attend(q_full, cos2, sin2, lat_blocks, order, w_uk, w_uv, heads, soft_scale, row, prompt, pairs, prior):
@@ -159,7 +176,7 @@
     last = n_tp - 1
     half = out.shape[1] // 2
     chunks = attn.shape[0] // size
-    skip = out.shape[0] - attn.shape[0]
+    skip = x_rows.shape[0] - attn.shape[0]
     got = (got_up, got_dn)
     place = (z, last - z)
     ahead = (z + 1, z - 1)
@@ -183,18 +200,22 @@
         pl.semaphore_wait(barrier, 1)
 
     def w_copy(i):
-        cols = pl.ds(i * tile, tile)
+        cols = pl.ds(i * tile if isinstance(i, int) else pl.multiple_of(i * tile, tile), tile)
         return pltpu.make_async_copy(w_o.at[:, cols], w_v.at[:, cols], w_sem.at[i])
 
     tiles = w_sem.shape[0]
-    for i in range(tiles // 2):
-        w_copy(i).start()
-        w_copy(tiles // 2 + i).start()
+    second = list(range(tiles // 2, tiles))
+    first = list(range(tiles // 2))
+    for near, wanted in ((z <= last // 2, second + first), (z > last // 2, first + second)):
+        @pl.when(near)
+        def _():
+            for i in wanted:
+                w_copy(i).start()
 
     def rows_of(u):
         return pl.ds(pl.multiple_of(u * size, size), size)
 
-    def out_rows(u):
+    def x_rows_of(u):
         return pl.ds(pl.multiple_of(skip + u * size, size), size)
 
     def a_copy(d, u):
@@ -205,11 +226,11 @@
         return pltpu.make_async_copy(got[d].at[rows_of(u)], r_v.at[d], r_sem.at[d])
 
     def x_copy(d, u):
-        return pltpu.make_async_copy(x_rows.at[out_rows(u), pl.ds(first_col[d], half)], x_v.at[d], x_sem.at[d])
+        return pltpu.make_async_copy(x_rows.at[x_rows_of(u), pl.ds(first_col[d], half)], x_v.at[d], x_sem.at[d])
 
     def f_copy(d, u):
         slot = lax.rem(u, 2)
-        return pltpu.make_async_copy(f_v.at[d, slot], out.at[out_rows(u), pl.ds(first_col[d], half)],
+        return pltpu.make_async_copy(f_v.at[d, slot], out.at[rows_of(u), pl.ds(first_col[d], half)],
                                      f_sem.at[d, slot])
 
     def sum_send(d, u):
@@ -220,12 +241,12 @@
 
     def res_first(d, u):
         return pltpu.make_async_remote_copy(
-            src_ref=f_v.at[d, lax.rem(u, 2)], dst_ref=out.at[out_rows(u), pl.ds(first_col[d], half)],
+            src_ref=f_v.at[d, lax.rem(u, 2)], dst_ref=out.at[rows_of(u), pl.ds(first_col[d], half)],
             send_sem=res_sent.at[d, u], recv_sem=res_got.at[d, u],
             device_id={'tp': behind[d]}, device_id_type=pl.DeviceIdType.MESH)
 
     def res_pass(d, u):
-        here = out.at[out_rows(u), pl.ds(first_col[d], half)]
+        here = out.at[rows_of(u), pl.ds(first_col[d], half)]
         return pltpu.make_async_remote_copy(
             src_ref=here, dst_ref=here, send_sem=res_sent.at[d, u], recv_sem=res_got.at[d, u],
             device_id={'tp': behind[d]}, device_id_type=pl.DeviceIdType.MESH)
@@ -279,11 +300,6 @@
                 res_pass(d, v).wait_recv()
                 res_pass(d, v).start()
 
-        @pl.when(t == -1)
-        def _():
-            for i in range(tiles):
-                w_copy(i).wait()
-
         for d in range(2):
             u = chunk[d]
 
@@ -309,6 +325,11 @@
                 def column_tile(j, carry):
                     cols = pl.ds(pl.multiple_of(j * tile, tile), tile)
                     w_cols = pl.ds(pl.multiple_of(first_col[d] + j * tile, tile), tile)
+
+                    @pl.when(u == -1)
+                    def _():
+                        w_copy(first_col[d] // tile + j).wait()
+
                     p_v[d, slot, :, cols] = jnp.dot(a_v[d, slot], w_v[:, w_cols], preferred_element_type=jnp.float32)
                     return carry
 
@@ -350,7 +371,7 @@
     sems = pltpu.SemaphoreType.DMA
     out, _, _ = pl.pallas_call(
         functools.partial(chain_kernel, n_tp, size),
-        out_shape=(jax.ShapeDtypeStruct(x_rows.shape, jnp.bfloat16),
+        out_shape=(jax.ShapeDtypeStruct((rows, width), jnp.bfloat16),
                    jax.ShapeDtypeStruct((rows, half), jnp.float32),
                    jax.ShapeDtypeStruct((rows, half), jnp.float32)),
         in_specs=[pl.BlockSpec(memory_space=pl.ANY)] * 3,
@@ -388,7 +409,6 @@
         n_blocks = 2 * n_cp
         block_len = seq_dev // 2
         n_pairs = heads_dev // PAIR
-        cuts = [n_pairs * i // SPLITS for i in range(SPLITS + 1)]
         pos_f32 = pos_blk.astype(jnp.float32)
         x_flat = x_blk.reshape(num_seq * seq_dev, width)
 
@@ -413,28 +433,25 @@
             q_latent = jnp.dot(rows, w_dq, preferred_element_type=jnp.float32).astype(jnp.bfloat16)
             return jnp.dot(rms_norm(q_latent, g_q), w_uq, preferred_element_type=jnp.float32).astype(jnp.bfloat16)
 
-        x_first, x_rest = x_flat[:seq_dev], x_flat[seq_dev:]
         everyone, order = gather(0, 1)
         everyone_r, order_r = gather(1, num_seq)
-        attn = attend(q_of(x_first), *tables, everyone, order[0], w_uk, w_uv, heads_dev, soft_scale, 0, 0,
+        attn = attend(q_of(x_flat[:seq_dev]), *tables, everyone, order[0], w_uk, w_uv, heads_dev, soft_scale, 0, 0,
                       range(n_pairs), None)
         share = jnp.dot(attn, w_o, preferred_element_type=jnp.float32)
-        x_rest, share = together(x_rest, share)
+        x_flat, share = together(x_flat, share)
         mine = lax.psum_scatter(share, 'tp', scatter_dimension=0, tiled=True)
-        q_rest = q_of(x_rest)
+        q_rest = q_of(x_flat[seq_dev:])
         attn = None
         for n in range(num_seq - 1):
-            for i in range(SPLITS):
-                attn = attend(q_rest, *tables, everyone_r, order_r[n], w_uk, w_uv, heads_dev, soft_scale, n, n + 1,
-                              range(cuts[i], cuts[i + 1]), attn)
-                if n == num_seq - 2 and i == 0:
-                    attn, mine = together(attn, mine)
-                    own = mine.shape[0]
-                    x_own = lax.dynamic_slice(x_first, (lax.axis_index('tp') * own, 0), (own, width))
-                    first_own = (x_own.astype(jnp.float32) + mine).astype(jnp.bfloat16)
-                    out_first = lax.all_gather(first_own, 'tp', axis=0, tiled=True)
-        out = chain_sum(attn, w_o, x_flat, n_tp, CHUNK)
-        out = lax.dynamic_update_slice(out, out_first, (0, 0)).reshape(x_blk.shape)
+            attn = attend(q_rest, *tables, everyone_r, order_r[n], w_uk, w_uv, heads_dev, soft_scale, n, n + 1,
+                          range(n_pairs), attn)
+        attn, mine = together(attn, mine)
+        own = mine.shape[0]
+        x_own = lax.dynamic_slice(x_flat, (lax.axis_index('tp') * own, 0), (own, width))
+        first_own = (x_own.astype(jnp.float32) + mine).astype(jnp.bfloat16)
+        out_first = lax.all_gather(first_own, 'tp', axis=0, tiled=True)
+        out_rest = chain_sum(attn, w_o, x_flat, n_tp, CHUNK)
+        out = jnp.concatenate([out_first, out_rest], axis=0).reshape(x_blk.shape)
         return out, latent.reshape(num_seq, seq_dev, -1), k_rope.reshape(num_seq, seq_dev, -1)
 
     seq_spec = P('dp', 'cp', None)

time: 680 us -> 663 us (0.975)
  local copies, waits for them, and re-layouts: 28.4 us -> 1.63 us
  waiting for transfers between devices: 16 us -> 0.11 us
  other arithmetic: 13.8 us -> 26.1 us
  Pallas kernels: 500 us -> 512 us
    pallas_call x1, Pallas kernels: 329 us -> 362 us  [chain_sum(): pl.pallas_call(functools.partial(chain_kernel, n_tp, size), out_shape=(ja...]
    pallas_call x7 -> x3, Pallas kernels: 172 us -> 150 us  [attend(): pl.pallas_call(functools.partial(attend_kernel, soft_scale, row), out_sha...]
    reduce_scatter x1, waiting for transfers between devices: 15.9 us -> 0.02 us  [local_step(): mine = lax.psum_scatter(share, 'tp', scatter_dimension=0, tiled=True)]
    slice x3 -> x0, local copies, waits for them, and re-layouts: 12.5 us -> none  [the longest x2 11.5 us: local_step(): x_first, x_rest = (x_flat[:seq_dev], x_flat[seq_dev:])]
    concatenate x0 -> x1, other arithmetic: none -> 10.5 us  [local_step(): out = jnp.concatenate([out_first, out_rest], axis=0).reshape(x_blk.shape)]
    unnamed x33 -> x18, local copies, waits for them, and re-layouts: 10.1 us -> 0.04 us
  transfers between devices with their start and end apart: 4 -> 4, of which waited for: 1 -> 0; matrix products, arithmetic and copies ran while one was open for 15% -> 15% of each run, Pallas kernels for 74% -> 77%
where the time goes in v3:
time: 663 us; the launch traced here: 661 us
  Pallas kernels  512 us (77%)
  matrix products  105 us (16%)
  other arithmetic  26.1 us (4%)
  between operations  16 us (2%)
    pallas_call x1, Pallas kernels, chain_sum(): pl.pallas_call(functools.partial(chain_kernel, n_tp, size), out_shape=(ja...  362 us
    pallas_call x3, Pallas kernels, attend(): pl.pallas_call(functools.partial(attend_kernel, soft_scale, row), out_sha...  150 us
    dot_general x2, matrix products, q_of(): jnp.dot(rms_norm(q_latent, g_q), w_uq, preferred_element_type=jnp.float32)  35.5 us
    dot_general x2, matrix products, q_of(): jnp.dot(rows, w_dq, preferred_element_type=jnp.float32).astype(jnp.bfloat16)  29 us
    dot_general x1, matrix products, local_step(): share = jnp.dot(attn, w_o, preferred_element_type=jnp.float32)  26.5 us
    dot_general x1, matrix products, local_step(): jnp.dot(x_flat, w_dkv, preferred_element_type=jnp.float32)  14 us
  transfers between devices with their start and end apart: 4, of which 0 were waited for; matrix products, arithmetic and copies ran while one was open for 15% of the time, Pallas kernels for 77%

profile of v3, /device:TPU:0, one launch (start us, length us, event | category | flops | bytes accessed | tf_op | source)
XLA Modules:
  0.0 661.4 jit_solution(375588790713871888)
XLA Ops:
  7.2 0.5 multiply_power_fusion
  7.7 14.0 %convolution_convert_fusion.2 = bf16[1152,576]{1,0:T(8,128)(2,1)S(1)} fusion(bf16[1152,5120]{1,0:T(8,128)(2,1)} %bitcast.35, bf16[5120,576]{0,1:T(8,128)(2,1)} %param.15), kind=kOutput, calls=%fused_computation.14 | convolution fusion | flops 6795436032 | bytes 19021824 | tf_op jit(solution)/shard_map/dot_general | solution.py:417
  21.7 0.3 fusion.14
  22.1 0.3 fusion.16
  22.5 4.1 fusion.26
  26.6 0.2 broadcast_in_dim.18
  26.8 0.9 pad_maximum_fusion.6
  27.8 1.2 pad_maximum_fusion.1
  29.0 0.2 reduce-scatter.2.cloned.1.call-start
  29.2 0.5 slice.58
  31.7 11.0 %fusion.17 = (f32[384]{0:T(512)S(1)}, bf16[384,1536]{1,0:T(8,128)(2,1)S(1)}) fusion(bf16[5120,1536]{1,0:T(8,128)(2,1)} %param.12, bf16[3,384,5120]{2,1,0:T(8,128)(2,1)} %param.10), kind=kOutput, calls=%fused_computation.23 | convolution fusion | flops 6042156544 | bytes 20841984 | tf_op jit(solution)/shard_map/dot_general | solution.py:433
  42.8 1.4 pad_maximum_fusion.4
  44.2 15.7 %convolution_convert_fusion.1.q_ref = bf16[384,6144]{1,0:T(8,128)(2,1)} fusion(bf16[1536,6144]{1,0:T(8,128)(2,1)} %param.14, bf16[384,1536]{1,0:T(8,128)(2,1)S(1)} %get-tuple-element.23, f32[1536]{0:T(1024)S(1)} %copy-done.8, f32[384]{0:T(512)S(1)} %add_rsqrt_fusion.2), kind=kOutput, calls=%fused_computation.2 | convolution fusion | flops 7252475904 | bytes 24780288 | tf_op jit(solution)/shard_map/dot_general | solution.py:434
  59.9 1.0 fusion.34
  60.9 0.1 select_reduce_fusion.1
  61.1 0.6 add_bitcast_fusion.order_ref
  61.6 50.0 %attend.3 = bf16[384,4096]{1,0:T(8,128)(2,1)} custom-call(s32[9]{0:T(128)} %add_bitcast_fusion.order_ref, bf16[384,6144]{1,0:T(8,128)(2,1)} %convolution_convert_fusion.1.q_ref, f32[1152,64]{1,0:T(8,128)} %get-tuple-element.26.cos_ref, f32[1152,64]{1,0:T(8,128)} %get-tuple-element.27.sin_ref, bf16[1,8,192,640]{3,2,1,0:T(8,128)(2,1)} %bitcast.43, ...), custom_call_target="tpu_custom_call" | custom-call | flops 21944598528 | bytes 18219008 | tf_op jit(solution)/shard_map/attend/pallas_call | solution.py:151
  111.6 26.5 %fusion.35 = f32[384,5120]{1,0:T(8,128)} fusion(bf16[384,4096]{1,0:T(8,128)(2,1)} %attend.3, bf16[4096,5120]{1,0:T(8,128)(2,1)} %w_o.1), kind=kOutput, calls=%fused_computation.66 | convolution fusion | flops 16106127360 | bytes 52953088 | tf_op jit(solution)/shard_map/dot_general | solution.py:440
  138.2 18.0 %fusion.2 = (f32[768]{0:T(1024)S(1)}, bf16[768,1536]{1,0:T(8,128)(2,1)S(1)}) fusion(bf16[5120,1536]{1,0:T(8,128)(2,1)} %param.12, bf16[1152,5120]{1,0:T(8,128)(2,1)} %bitcast.36), kind=kOutput, calls=%fused_computation.7 | convolution fusion | flops 12084313088 | bytes 25955328 | tf_op jit(solution)/shard_map/dot_general | solution.py:433
  156.2 19.7 %convolution_convert_fusion.q_ref = bf16[768,6144]{1,0:T(8,128)(2,1)} fusion(bf16[1536,6144]{1,0:T(8,128)(2,1)} %param.14, bf16[768,1536]{1,0:T(8,128)(2,1)S(1)} %get-tuple-element.25, f32[1536]{0:T(1024)S(1)} %copy-done.8, f32[768]{0:T(1024)S(1)} %add_rsqrt_fusion.1), kind=kOutput, calls=%fused_computation.1 | convolution fusion | flops 14504951808 | bytes 30680064 | tf_op jit(solution)/shard_map/dot_general | solution.py:434
  176.0 1.2 fusion.33
  177.2 0.2 select_reduce_fusion
  177.3 0.1 pad_add_fusion
  177.4 0.5 slice_bitcast_fusion
  177.9 50.0 %attend.4.rest_0_ = bf16[768,4096]{1,0:T(8,128)(2,1)} custom-call(s32[9]{0:T(128)} %get-tuple-element.20.order_ref, bf16[768,6144]{1,0:T(8,128)(2,1)} %convolution_convert_fusion.q_ref, f32[1152,64]{1,0:T(8,128)} %get-tuple-element.26.cos_ref, f32[1152,64]{1,0:T(8,128)} %get-tuple-element.27.sin_ref, bf16[2,8,192,640]{3,2,1,0:T(8,128)(2,1)} %bitcast.40, ...), custom_call_target="tpu_custom_call" | custom-call | flops 21944598528 | bytes 18219008 | tf_op jit(solution)/shard_map/attend/pallas_call | solution.py:151
  228.0 50.1 %attend.5.attn = bf16[768,4096]{1,0:T(8,128)(2,1)} custom-call(s32[9]{0:T(128)} %get-tuple-element.21.order_ref, bf16[768,6144]{1,0:T(8,128)(2,1)} %convolution_convert_fusion.q_ref, f32[1152,64]{1,0:T(8,128)} %get-tuple-element.26.cos_ref, f32[1152,64]{1,0:T(8,128)} %get-tuple-element.27.sin_ref, ...), custom_call_target="tpu_custom_call", output_to_operand_aliasing={{}: (7, {})} | custom-call | flops 21944598528 | bytes 18219008 | tf_op jit(solution)/shard_map/attend/pallas_call | solution.py:151
  278.1 3.0 add_convert_fusion
  281.1 0.2 copy.21
  281.3 0.2 copy.22
  281.4 0.7 pad_maximum_fusion.7
  282.1 362.2 %chain_sum.1 = (bf16[768,5120]{1,0:T(8,128)(2,1)}, f32[768,2560]{1,0:T(8,128)}, f32[768,2560]{1,0:T(8,128)}) custom-call(bf16[768,4096]{1,0:T(8,128)(2,1)} %attend.5.attn, bf16[4096,5120]{1,0:T(8,128)(2,1)} %w_o.1, bf16[1152,5120]{1,0:T(8,128)(2,1)} %bitcast.38), custom_call_target="tpu_custom_call" | custom-call | flops 32212254720 | bytes 89128960 | tf_op jit(solution)/shard_map/chain_sum/pallas_call | solution.py:372
  644.4 10.5 %pad_maximum_fusion = bf16[1152,5120]{1,0:T(8,128)(2,1)} fusion(bf16[768,5120]{1,0:T(8,128)(2,1)} %get-tuple-element.12, bf16[384,5120]{1,0:T(8,128)(2,1)} %all-gather.7.cloned.1.call-done), kind=kLoop, calls=%fused_computation | loop fusion | flops 23592960 | bytes 23592960 | tf_op jit(solution)/shard_map/concatenate | solution.py:454
  (37 shorter events, 0.4 us)
Async XLA Ops:
  7.2 52.7 %all-gather.9.cloned.1.call-start = ((), (), s32[]{:S(2)}) async-start(), calls=%async_computation.4 | async-start | bytes 2457600 | tf_op jit(solution)/shard_map/all_gather | solution.py:425
  7.7 14.3 %copy-start.6 = (s32[3,384]{1,0:T(4,128)S(1)}, s32[3,384]{1,0:T(4,128)}, u32[]{:S(2)}) copy-start(s32[3,384]{1,0:T(4,128)} %param.11) | copy-start | bytes 13828
  7.7 14.4 %copy-start.7 = (f32[512]{0:T(512)S(1)}, f32[512]{0:T(512)}, u32[]{:S(2)}) copy-start(f32[512]{0:T(512)} %param.16) | copy-start | bytes 6148
  22.5 6.5 copy-start
  26.6 16.2 %copy-start.1 = (bf16[1152,32]{1,0:T(8,128)(2,1)}, bf16[1152,32]{1,0:T(8,128)(2,1)S(1)}, u32[]{:S(2)}) copy-start(bf16[1152,32]{1,0:T(8,128)(2,1)S(1)} %get-tuple-element.17) | copy-start | bytes 221188
  26.6 16.2 %copy-start.3 = (bf16[1152,32]{1,0:T(8,128)(2,1)}, bf16[1152,32]{1,0:T(8,128)(2,1)S(1)}, u32[]{:S(2)}) copy-start(bf16[1152,32]{1,0:T(8,128)(2,1)S(1)} %get-tuple-element.18) | copy-start | bytes 221188
  27.7 148.2 %all-gather.5.cloned.1.call-start = ((), (), s32[]{:S(2)}) async-start(), calls=%async_computation.1 | async-start | bytes 4915200 | tf_op jit(solution)/shard_map/all_gather | solution.py:425
  29.0 249.1 %reduce-scatter.2.cloned.1.call-start = ((), (), s32[]{:S(2)}) async-start(), calls=%async_computation.2 | async-start | bytes 9830400 | tf_op jit(solution)/shard_map/reduce_scatter | solution.py:442
  31.7 11.1 %copy-start.5 = (f32[1152,32]{1,0:T(8,128)S(1)}, f32[1152,32]{1,0:T(8,128)}, u32[]{:S(2)}) copy-start(f32[1152,32]{1,0:T(8,128)} %get-tuple-element.19) | copy-start | bytes 442372
  31.7 12.5 %copy-start.8 = (f32[1536]{0:T(1024)S(1)}, f32[1536]{0:T(1024)}, u32[]{:S(2)}) copy-start(f32[1536]{0:T(1024)} %param.13) | copy-start | bytes 18436
  138.2 506.2 %all-gather.7.cloned.1.call-start = ((), (), s32[]{:S(2)}) async-start(), calls=%async_computation.3 | async-start | bytes 4915200 | tf_op jit(solution)/shard_map/all_gather | solution.py:452
  278.0 3.1 copy-start.4
  278.0 3.2 copy-start.2
Sparse Core Ops, SparseCore 0:
  27.8 24.3 all-gather.8
  53.8 32.8 all-gather.4
  138.3 138.7 reduce-scatter.1
  281.2 128.0 all-gather.6

commit v4 on v3

--- a/solution.py
+++ b/solution.py
@@ -10,7 +10,7 @@
 ROPE_BASE = 10000.0
 NORM_EPS = 1e-6
 LOG2_E = 1.4426950408889634
-CHUNK = 32
+CHUNK = 16
 LAG = 2
 LAG_BACK = 2
 PAIR = 2
@@ -218,9 +218,13 @@
     def x_rows_of(u):
         return pl.ds(pl.multiple_of(skip + u * size, size), size)
 
-    def a_copy(d, u):
-        slot = lax.rem(u, 2)
-        return pltpu.make_async_copy(attn.at[rows_of(u)], a_v.at[d, slot], a_sem.at[d, slot])
+    def a_copy(d, duo):
+        slot = lax.rem(duo, 2)
+        duo_rows = pl.ds(pl.multiple_of(duo * 2 * size, 2 * size), 2 * size)
+        return pltpu.make_async_copy(attn.at[duo_rows], a_v.at[d, slot], a_sem.at[d, slot])
+
+    def sum_at(d, u):
+        return p_v.at[d, lax.rem(lax.div(u, 2), 2), lax.rem(u, 2)]
 
     def r_copy(d, u):
         return pltpu.make_async_copy(got[d].at[rows_of(u)], r_v.at[d], r_sem.at[d])
@@ -235,7 +239,7 @@
 
     def sum_send(d, u):
         return pltpu.make_async_remote_copy(
-            src_ref=p_v.at[d, lax.rem(u, 2)], dst_ref=got[d].at[rows_of(u)],
+            src_ref=sum_at(d, u), dst_ref=got[d].at[rows_of(u)],
             send_sem=sum_sent.at[d, u], recv_sem=sum_got.at[d, u],
             device_id={'tp': ahead[d]}, device_id_type=pl.DeviceIdType.MESH)
 
@@ -271,7 +275,8 @@
 
         for d in range(2):
             u = chunk[d]
-            slot = lax.rem(u + 2, 2)
+            slot = lax.rem(jnp.maximum(u, 0), 2)
+            total = sum_at(d, jnp.maximum(u, 0))
 
             @pl.when(inside(u) & (place[d] > 0))
             def _():
@@ -279,7 +284,7 @@
 
             @pl.when(inside(u) & (place[d] > 0) & (place[d] < last))
             def _():
-                p_v[d, slot] = p_v[d, slot] + r_v[d]
+                total[...] = total[...] + r_v[d]
 
             @pl.when(inside(u) & (place[d] < last))
             def _():
@@ -288,7 +293,7 @@
             @pl.when(inside(u) & (place[d] == last))
             def _():
                 x_copy(d, u).wait()
-                f_v[d, slot] = (x_v[d].astype(jnp.float32) + (p_v[d, slot] + r_v[d])).astype(jnp.bfloat16)
+                f_v[d, slot] = (x_v[d].astype(jnp.float32) + (total[...] + r_v[d])).astype(jnp.bfloat16)
                 f_copy(d, u).start()
                 res_first(d, u).start()
 
@@ -303,24 +308,26 @@
         for d in range(2):
             u = chunk[d]
 
-            @pl.when(inside(u + 2))
-            def _():
-                a_copy(d, u + 2).start()
-
-            @pl.when(inside(u + 1))
-            def _():
-                slot = lax.rem(u + 1, 2)
-
-                @pl.when(inside(u - 1) & (place[d] < last))
+            @pl.when(inside(u + 1) & inside(u - 1) & (place[d] == last))
+            def _():
+                f_copy(d, u - 1).wait()
+                res_first(d, u - 1).wait_send()
+
+            @pl.when(inside(u + 2) & (lax.rem(t + 4, 2) == 0))
+            def _():
+                a_copy(d, lax.div(u + 2, 2)).start()
+
+            @pl.when(inside(u + 1) & (lax.rem(t + 4, 2) == 1))
+            def _():
+                duo = lax.div(u + 1, 2)
+                slot = lax.rem(duo, 2)
+
+                @pl.when(inside(u - 3) & (place[d] < last))
                 def _():
-                    sum_send(d, u - 1).wait_send()
-
-                @pl.when(inside(u - 1) & (place[d] == last))
-                def _():
-                    f_copy(d, u - 1).wait()
-                    res_first(d, u - 1).wait_send()
-
-                a_copy(d, u + 1).wait()
+                    sum_send(d, u - 3).wait_send()
+                    sum_send(d, u - 2).wait_send()
+
+                a_copy(d, duo).wait()
 
                 def column_tile(j, carry):
                     cols = pl.ds(pl.multiple_of(j * tile, tile), tile)
@@ -330,7 +337,9 @@
                     def _():
                         w_copy(first_col[d] // tile + j).wait()
 
-                    p_v[d, slot, :, cols] = jnp.dot(a_v[d, slot], w_v[:, w_cols], preferred_element_type=jnp.float32)
+                    both = jnp.dot(a_v[d, slot], w_v[:, w_cols], preferred_element_type=jnp.float32)
+                    p_v[d, slot, 0, :, cols] = both[:size]
+                    p_v[d, slot, 1, :, cols] = both[size:]
                     return carry
 
                 lax.fori_loop(0, tiles // 2, column_tile, 0)
@@ -339,11 +348,12 @@
     lax.fori_loop(0, chunks + 2 + LAG * last + LAG_BACK * (last - 1), step, 0)
 
     for d in range(2):
+        for u in range(chunks - 4, chunks):
+            @pl.when(place[d] < last)
+            def _():
+                sum_send(d, u).wait_send()
+
         for u in (chunks - 2, chunks - 1):
-            @pl.when(place[d] < last)
-            def _():
-                sum_send(d, u).wait_send()
-
             @pl.when(place[d] == last)
             def _():
                 f_copy(d, u).wait()
@@ -378,8 +388,8 @@
         out_specs=(pl.BlockSpec(memory_space=pl.ANY),) * 3,
         scratch_shapes=[
             pltpu.VMEM((inner, width), jnp.bfloat16),
-            pltpu.VMEM((2, 2, size, inner), jnp.bfloat16),
-            pltpu.VMEM((2, 2, size, half), jnp.float32),
+            pltpu.VMEM((2, 2, 2 * size, inner), jnp.bfloat16),
+            pltpu.VMEM((2, 2, 2, size, half), jnp.float32),
             pltpu.VMEM((2, size, half), jnp.float32),
             pltpu.VMEM((2, size, half), jnp.bfloat16),
             pltpu.VMEM((2, 2, size, half), jnp.bfloat16),

time: 663 us -> 671 us (1.012)
  Pallas kernels: 512 us -> 520 us
    pallas_call x1, Pallas kernels: 362 us -> 370 us  [chain_sum(): pl.pallas_call(functools.partial(chain_kernel, n_tp, size), out_shape=(ja...]
  transfers between devices with their start and end apart: 4 -> 4, of which waited for: 0 -> 0; matrix products, arithmetic and copies ran while one was open for 15% -> 15% of each run, Pallas kernels for 77% -> 78%
where the time goes in v4:
time: 671 us; the launch traced here: 669 us
  Pallas kernels  520 us (77%)
  matrix products  105 us (16%)
  other arithmetic  26.1 us (4%)
  between operations  16 us (2%)
    pallas_call x1, Pallas kernels, chain_sum(): pl.pallas_call(functools.partial(chain_kernel, n_tp, size), out_shape=(ja...  370 us
    pallas_call x3, Pallas kernels, attend(): pl.pallas_call(functools.partial(attend_kernel, soft_scale, row), out_sha...  150 us
    dot_general x2, matrix products, q_of(): jnp.dot(rms_norm(q_latent, g_q), w_uq, preferred_element_type=jnp.float32)  35.5 us
    dot_general x2, matrix products, q_of(): jnp.dot(rows, w_dq, preferred_element_type=jnp.float32).astype(jnp.bfloat16)  29 us
    dot_general x1, matrix products, local_step(): share = jnp.dot(attn, w_o, preferred_element_type=jnp.float32)  26.5 us
    dot_general x1, matrix products, local_step(): jnp.dot(x_flat, w_dkv, preferred_element_type=jnp.float32)  14 us
  transfers between devices with their start and end apart: 4, of which 0 were waited for; matrix products, arithmetic and copies ran while one was open for 15% of the time, Pallas kernels for 78%

profile of v4, /device:TPU:0, one launch (start us, length us, event | category | flops | bytes accessed | tf_op | source)
XLA Modules:
  0.0 668.7 jit_solution(13854912781293454209)
XLA Ops:
  7.2 0.5 multiply_power_fusion
  7.7 14.0 %convolution_convert_fusion.2 = bf16[1152,576]{1,0:T(8,128)(2,1)S(1)} fusion(bf16[1152,5120]{1,0:T(8,128)(2,1)} %bitcast.35, bf16[5120,576]{0,1:T(8,128)(2,1)} %param.15), kind=kOutput, calls=%fused_computation.14 | convolution fusion | flops 6795436032 | bytes 19021824 | tf_op jit(solution)/shard_map/dot_general | solution.py:427
  21.7 0.3 fusion.14
  22.1 0.3 fusion.16
  22.5 4.1 fusion.26
  26.6 0.2 broadcast_in_dim.18
  26.8 0.9 pad_maximum_fusion.6
  27.8 1.2 pad_maximum_fusion.1
  29.0 0.2 reduce-scatter.2.cloned.1.call-start
  29.2 0.5 slice.58
  31.7 11.0 %fusion.17 = (f32[384]{0:T(512)S(1)}, bf16[384,1536]{1,0:T(8,128)(2,1)S(1)}) fusion(bf16[5120,1536]{1,0:T(8,128)(2,1)} %param.12, bf16[3,384,5120]{2,1,0:T(8,128)(2,1)} %param.10), kind=kOutput, calls=%fused_computation.23 | convolution fusion | flops 6042156544 | bytes 20841984 | tf_op jit(solution)/shard_map/dot_general | solution.py:443
  42.8 1.4 pad_maximum_fusion.4
  44.2 15.7 %convolution_convert_fusion.1.q_ref = bf16[384,6144]{1,0:T(8,128)(2,1)} fusion(bf16[1536,6144]{1,0:T(8,128)(2,1)} %param.14, bf16[384,1536]{1,0:T(8,128)(2,1)S(1)} %get-tuple-element.23, f32[1536]{0:T(1024)S(1)} %copy-done.8, f32[384]{0:T(512)S(1)} %add_rsqrt_fusion.2), kind=kOutput, calls=%fused_computation.2 | convolution fusion | flops 7252475904 | bytes 24780288 | tf_op jit(solution)/shard_map/dot_general | solution.py:444
  59.9 1.0 fusion.34
  60.9 0.1 select_reduce_fusion.1
  61.1 0.6 add_bitcast_fusion.order_ref
  61.6 50.0 %attend.3 = bf16[384,4096]{1,0:T(8,128)(2,1)} custom-call(s32[9]{0:T(128)} %add_bitcast_fusion.order_ref, bf16[384,6144]{1,0:T(8,128)(2,1)} %convolution_convert_fusion.1.q_ref, f32[1152,64]{1,0:T(8,128)} %get-tuple-element.26.cos_ref, f32[1152,64]{1,0:T(8,128)} %get-tuple-element.27.sin_ref, bf16[1,8,192,640]{3,2,1,0:T(8,128)(2,1)} %bitcast.43, ...), custom_call_target="tpu_custom_call" | custom-call | flops 21944598528 | bytes 18219008 | tf_op jit(solution)/shard_map/attend/pallas_call | solution.py:151
  111.6 26.5 %fusion.35 = f32[384,5120]{1,0:T(8,128)} fusion(bf16[384,4096]{1,0:T(8,128)(2,1)} %attend.3, bf16[4096,5120]{1,0:T(8,128)(2,1)} %w_o.1), kind=kOutput, calls=%fused_computation.66 | convolution fusion | flops 16106127360 | bytes 52953088 | tf_op jit(solution)/shard_map/dot_general | solution.py:450
  138.2 18.0 %fusion.2 = (f32[768]{0:T(1024)S(1)}, bf16[768,1536]{1,0:T(8,128)(2,1)S(1)}) fusion(bf16[5120,1536]{1,0:T(8,128)(2,1)} %param.12, bf16[1152,5120]{1,0:T(8,128)(2,1)} %bitcast.36), kind=kOutput, calls=%fused_computation.7 | convolution fusion | flops 12084313088 | bytes 25955328 | tf_op jit(solution)/shard_map/dot_general | solution.py:443
  156.2 19.7 %convolution_convert_fusion.q_ref = bf16[768,6144]{1,0:T(8,128)(2,1)} fusion(bf16[1536,6144]{1,0:T(8,128)(2,1)} %param.14, bf16[768,1536]{1,0:T(8,128)(2,1)S(1)} %get-tuple-element.25, f32[1536]{0:T(1024)S(1)} %copy-done.8, f32[768]{0:T(1024)S(1)} %add_rsqrt_fusion.1), kind=kOutput, calls=%fused_computation.1 | convolution fusion | flops 14504951808 | bytes 30680064 | tf_op jit(solution)/shard_map/dot_general | solution.py:444
  176.0 1.2 fusion.33
  177.2 0.2 select_reduce_fusion
  177.3 0.1 pad_add_fusion
  177.4 0.5 slice_bitcast_fusion
  177.9 50.0 %attend.4.rest_0_ = bf16[768,4096]{1,0:T(8,128)(2,1)} custom-call(s32[9]{0:T(128)} %get-tuple-element.20.order_ref, bf16[768,6144]{1,0:T(8,128)(2,1)} %convolution_convert_fusion.q_ref, f32[1152,64]{1,0:T(8,128)} %get-tuple-element.26.cos_ref, f32[1152,64]{1,0:T(8,128)} %get-tuple-element.27.sin_ref, bf16[2,8,192,640]{3,2,1,0:T(8,128)(2,1)} %bitcast.40, ...), custom_call_target="tpu_custom_call" | custom-call | flops 21944598528 | bytes 18219008 | tf_op jit(solution)/shard_map/attend/pallas_call | solution.py:151
  228.0 50.1 %attend.5.attn = bf16[768,4096]{1,0:T(8,128)(2,1)} custom-call(s32[9]{0:T(128)} %get-tuple-element.21.order_ref, bf16[768,6144]{1,0:T(8,128)(2,1)} %convolution_convert_fusion.q_ref, f32[1152,64]{1,0:T(8,128)} %get-tuple-element.26.cos_ref, f32[1152,64]{1,0:T(8,128)} %get-tuple-element.27.sin_ref, ...), custom_call_target="tpu_custom_call", output_to_operand_aliasing={{}: (7, {})} | custom-call | flops 21944598528 | bytes 18219008 | tf_op jit(solution)/shard_map/attend/pallas_call | solution.py:151
  278.1 3.0 add_convert_fusion
  281.1 0.2 copy.21
  281.3 0.2 copy.22
  281.4 0.7 pad_maximum_fusion.7
  282.1 369.5 %chain_sum.1 = (bf16[768,5120]{1,0:T(8,128)(2,1)}, f32[768,2560]{1,0:T(8,128)}, f32[768,2560]{1,0:T(8,128)}) custom-call(bf16[768,4096]{1,0:T(8,128)(2,1)} %attend.5.attn, bf16[4096,5120]{1,0:T(8,128)(2,1)} %w_o.1, bf16[1152,5120]{1,0:T(8,128)(2,1)} %bitcast.38), custom_call_target="tpu_custom_call" | custom-call | flops 32212254720 | bytes 89128960 | tf_op jit(solution)/shard_map/chain_sum/pallas_call | solution.py:382
  651.7 10.5 %pad_maximum_fusion = bf16[1152,5120]{1,0:T(8,128)(2,1)} fusion(bf16[768,5120]{1,0:T(8,128)(2,1)} %get-tuple-element.12, bf16[384,5120]{1,0:T(8,128)(2,1)} %all-gather.7.cloned.1.call-done), kind=kLoop, calls=%fused_computation | loop fusion | flops 23592960 | bytes 23592960 | tf_op jit(solution)/shard_map/concatenate | solution.py:464
  (37 shorter events, 0.4 us)
Async XLA Ops:
  7.2 52.7 %all-gather.9.cloned.1.call-start = ((), (), s32[]{:S(2)}) async-start(), calls=%async_computation.4 | async-start | bytes 2457600 | tf_op jit(solution)/shard_map/all_gather | solution.py:435
  7.7 14.3 %copy-start.6 = (s32[3,384]{1,0:T(4,128)S(1)}, s32[3,384]{1,0:T(4,128)}, u32[]{:S(2)}) copy-start(s32[3,384]{1,0:T(4,128)} %param.11) | copy-start | bytes 13828
  7.7 14.4 %copy-start.7 = (f32[512]{0:T(512)S(1)}, f32[512]{0:T(512)}, u32[]{:S(2)}) copy-start(f32[512]{0:T(512)} %param.16) | copy-start | bytes 6148
  22.5 6.5 copy-start
  26.6 16.2 %copy-start.1 = (bf16[1152,32]{1,0:T(8,128)(2,1)}, bf16[1152,32]{1,0:T(8,128)(2,1)S(1)}, u32[]{:S(2)}) copy-start(bf16[1152,32]{1,0:T(8,128)(2,1)S(1)} %get-tuple-element.17) | copy-start | bytes 221188
  26.6 16.2 %copy-start.3 = (bf16[1152,32]{1,0:T(8,128)(2,1)}, bf16[1152,32]{1,0:T(8,128)(2,1)S(1)}, u32[]{:S(2)}) copy-start(bf16[1152,32]{1,0:T(8,128)(2,1)S(1)} %get-tuple-element.18) | copy-start | bytes 221188
  27.7 148.2 %all-gather.5.cloned.1.call-start = ((), (), s32[]{:S(2)}) async-start(), calls=%async_computation.1 | async-start | bytes 4915200 | tf_op jit(solution)/shard_map/all_gather | solution.py:435
  29.0 249.1 %reduce-scatter.2.cloned.1.call-start = ((), (), s32[]{:S(2)}) async-start(), calls=%async_computation.2 | async-start | bytes 9830400 | tf_op jit(solution)/shard_map/reduce_scatter | solution.py:452
  31.7 11.1 %copy-start.5 = (f32[1152,32]{1,0:T(8,128)S(1)}, f32[1152,32]{1,0:T(8,128)}, u32[]{:S(2)}) copy-start(f32[1152,32]{1,0:T(8,128)} %get-tuple-element.19) | copy-start | bytes 442372
  31.7 12.5 %copy-start.8 = (f32[1536]{0:T(1024)S(1)}, f32[1536]{0:T(1024)}, u32[]{:S(2)}) copy-start(f32[1536]{0:T(1024)} %param.13) | copy-start | bytes 18436
  138.2 513.5 %all-gather.7.cloned.1.call-start = ((), (), s32[]{:S(2)}) async-start(), calls=%async_computation.3 | async-start | bytes 4915200 | tf_op jit(solution)/shard_map/all_gather | solution.py:462
  278.0 3.1 copy-start.4
  278.0 3.2 copy-start.2
Sparse Core Ops, SparseCore 0:
  27.8 24.3 all-gather.8
  53.8 32.8 all-gather.4
  138.3 138.7 reduce-scatter.1
  281.2 128.0 all-gather.6
